TPU v7x, 32 devices: a whole 2x2x4 slice. The times are simulated.
32 devices in a mesh: data: 32 (over z, y, x, core).
Axes of the slice: x: 2, y: 2, z: 4, core: 2. Of those that a mesh axis runs over, the one named last changes fastest.
Arguments:
- h_a: bfloat16 [16384, 2048], P('data')
- h_b: bfloat16 [16384, 2048], P('data')
- w_one: bfloat16 [2048, 2048], replicated
- w_two: bfloat16 [2048, 2048], replicated
- w_three: bfloat16 [2048, 2048], replicated
- gain_one: float32 [2048], replicated
- shift_one: float32 [2048], replicated
- gain_two: float32 [2048], replicated
- shift_two: float32 [2048], replicated
- lam_off: float32 [], replicated
Outputs:
- output 1: float32 [], replicated
- output 2: float32 [2048, 2048], P('data')
- output 3: float32 [2048, 2048], P('data')
- output 4: float32 [2048, 2048], P('data')
- output 5: float32 [2048], replicated
- output 6: float32 [2048], replicated
- output 7: float32 [2048], replicated
- output 8: float32 [2048], replicated
All inputs are finite; a program needn't handle non-finite values.
Results may differ from a plain program's by a relative error of at most 0.00508914.
Values are sent between devices in bfloat16 or wider.
A program may use at most 1 GiB of HBM per device.

v0:
```python
import jax
import jax.numpy as jnp
from jax import lax
from jax.sharding import PartitionSpec as P

NORM_EPS = 1e-5
ROW_DIMS = (((0, 1), (0, 1)), ((), ()))
FIRST_DIMS = (((0,), (0,)), ((), ()))
LAST_DIMS = (((2,), (1,)), ((), ()))


def norm_forward(values, total_rows):
    col_sums = jnp.stack([jnp.sum(values, axis=1), jnp.sum(values * values, axis=1)])
    col_sums = lax.psum(col_sums, "data")
    col_mean = col_sums[0] / total_rows
    inv_std = lax.rsqrt(col_sums[1] / total_rows - col_mean * col_mean + NORM_EPS)
    return (values - col_mean[:, None, :]) * inv_std[:, None, :], inv_std


def norm_backward(grad_out, normed, inv_std, total_rows):
    col_sums = lax.psum(jnp.stack([jnp.sum(grad_out, axis=1), jnp.sum(grad_out * normed, axis=1)]), "data")
    grad_in = inv_std[:, None, :] * (grad_out - (col_sums[0][:, None, :] + normed * col_sums[1][:, None, :]) / total_rows)
    return grad_in, col_sums


def solution(mesh):
    shards = mesh.shape["data"]

    def local_step(h_a, h_b, w_one, w_two, w_three, gain_one, shift_one, gain_two, shift_two, lam_off):
        rows_dev = h_a.shape[0]
        total_rows = rows_dev * shards
        feat_rows = jnp.concatenate([h_a, h_b], axis=0)
        hidden_one = jnp.dot(feat_rows, w_one, preferred_element_type=jnp.float32).reshape(2, rows_dev, -1)
        normed_one, inv_one = norm_forward(hidden_one, total_rows)
        pre_one = gain_one * normed_one + shift_one
        act_one = jax.nn.relu(pre_one).astype(jnp.bfloat16)
        hidden_two = jnp.dot(act_one, w_two, preferred_element_type=jnp.float32)
        normed_two, inv_two = norm_forward(hidden_two, total_rows)
        pre_two = gain_two * normed_two + shift_two
        act_two = jax.nn.relu(pre_two).astype(jnp.bfloat16)
        proj_out = jnp.dot(act_two, w_three, preferred_element_type=jnp.float32)
        normed_out, inv_out = norm_forward(proj_out, total_rows)
        embed_pair = normed_out.astype(jnp.bfloat16)
        corr_part = lax.dot_general(embed_pair[0], embed_pair[1], FIRST_DIMS, preferred_element_type=jnp.float32)
        corr_mat = lax.psum(corr_part, "data") / total_rows
        feat_index = jnp.arange(corr_mat.shape[0])
        diag_mask = feat_index[:, None] == feat_index[None, :]
        diag_gap = 1.0 - corr_mat
        loss_total = jnp.sum(jnp.where(diag_mask, diag_gap * diag_gap, lam_off * corr_mat * corr_mat))
        grad_corr = jnp.where(diag_mask, -2.0 * diag_gap, 2.0 * lam_off * corr_mat)
        grad_scaled = (grad_corr / total_rows).astype(jnp.bfloat16)
        grad_embed_a = lax.dot_general(embed_pair[1], grad_scaled, (((1,), (1,)), ((), ())),
                                       preferred_element_type=jnp.float32)
        grad_embed_b = jnp.dot(embed_pair[0], grad_scaled, preferred_element_type=jnp.float32)
        grad_embed = jnp.stack([grad_embed_a, grad_embed_b])
        grad_proj = norm_backward(grad_embed, normed_out, inv_out, total_rows)[0].astype(jnp.bfloat16)
        grad_w_three = lax.psum_scatter(
            lax.dot_general(act_two, grad_proj, ROW_DIMS, preferred_element_type=jnp.float32),
            "data", scatter_dimension=0, tiled=True)
        grad_act_two = lax.dot_general(grad_proj, w_three, LAST_DIMS, preferred_element_type=jnp.float32)
        grad_pre_two = jnp.where(pre_two > 0, grad_act_two, 0.0)
        grad_hidden_two, sums_two = norm_backward(grad_pre_two, normed_two, inv_two, total_rows)
        grad_hidden_two = (gain_two * grad_hidden_two).astype(jnp.bfloat16)
        grad_w_two = lax.psum_scatter(
            lax.dot_general(act_one, grad_hidden_two, ROW_DIMS, preferred_element_type=jnp.float32),
            "data", scatter_dimension=0, tiled=True)
        grad_act_one = lax.dot_general(grad_hidden_two, w_two, LAST_DIMS, preferred_element_type=jnp.float32)
        grad_pre_one = jnp.where(pre_one > 0, grad_act_one, 0.0)
        grad_hidden_one, sums_one = norm_backward(grad_pre_one, normed_one, inv_one, total_rows)
        grad_hidden_one = (gain_one * grad_hidden_one).astype(jnp.bfloat16).reshape(2 * rows_dev, -1)
        grad_w_one = lax.psum_scatter(
            lax.dot_general(feat_rows, grad_hidden_one, FIRST_DIMS, preferred_element_type=jnp.float32),
            "data", scatter_dimension=0, tiled=True)
        return (loss_total, grad_w_one, grad_w_two, grad_w_three,
                jnp.sum(sums_one[1], axis=0), jnp.sum(sums_one[0], axis=0),
                jnp.sum(sums_two[1], axis=0), jnp.sum(sums_two[0], axis=0))

    row_spec = P("data", None)
    whole_mat = P(None, None)
    whole_vec = P(None)
    return jax.shard_map(
        local_step, mesh=mesh,
        in_specs=(row_spec, row_spec, whole_mat, whole_mat, whole_mat,
                  whole_vec, whole_vec, whole_vec, whole_vec, P()),
        out_specs=(P(), row_spec, row_spec, row_spec, whole_vec, whole_vec, whole_vec, whole_vec),
        check_vma=False)
```

profile of v0, /device:TPU:0, one launch (start us, length us, event | category | flops | bytes accessed | tf_op | source)
XLA Modules:
  0.0 1130.4 jit_solution(8215530697780934731)
XLA Ops:
  7.2 0.0 all-reduce.2.cloned.1.call-start
  7.2 1.7 constant_dynamic-update-slice_fusion.1
  8.9 1.7 constant_dynamic-update-slice_fusion
  10.7 0.0 copy-start.4
  10.7 0.0 copy-start.7
  10.7 0.0 copy-start.9
  10.7 14.8 %bitcast_reduce_fusion = (f32[2,2048]{1,0:T(2,128)S(1)}, f32[2,2048]{1,0:T(2,128)S(1)}, f32[1024,2048]{1,0:T(8,128)}) fusion(bf16[1024,2048]{1,0:T(8,128)(2,1)S(1)} %constant_dynamic-update-slice_fusion, bf16[2048,2048]{1,0:T(8,128)(2,1)} %param.12), kind=kOutput, calls=%fused_computation.16 | convolution fusion | flops 8596217856 | bytes 21004288 | tf_op jit(solution)/shard_map/dot_general | solution.py:33
  25.5 42.1 %psum.49 = f32[2,2,2048]{2,1,0:T(2,128)S(1)} all-reduce(f32[2,2,2048]{2,1,0:T(2,128)S(1)} %pad_maximum_fusion.1), channel_id=1, replica_groups=mesh['data'=32] {'data'}, use_global_device_ids=true, to_apply=%region_2.0 | all-reduce | flops 8192 | bytes 65536 | tf_op jit(solution)/shard_map/psum | solution.py:14
  67.7 0.0 copy-start.6
  67.7 0.0 copy-start.8
  67.7 15.9 %fusion.35 = (f32[2,2048]{1,0:T(2,128)S(1)}, f32[2,2048]{1,0:T(2,128)S(1)}, f32[2,512,2048]{2,1,0:T(8,128)}) fusion(bf16[2048,2048]{1,0:T(8,128)(2,1)} %param.13, f32[1024,2048]{1,0:T(8,128)} %get-tuple-element.30, f32[2048]{0:T(1024)S(1)} %copy-done.9, f32[2,2048]{1,0:T(2,128)S(1)} %fusion.30, f32[2,2048]{1,0:T(2,128)S(1)} %fusion.31, f32[2048]{0:T(1024)S(1)} %copy-done.7), kind=kOutput, calls=%fused_computation.84 | convolution fusion | flops 8608800768 | bytes 25247744 | tf_op jit(solution)/shard_map/dot_general | solution.py:37
  83.6 40.9 %psum.50 = f32[2,2,2048]{2,1,0:T(2,128)S(1)} all-reduce(f32[2,2,2048]{2,1,0:T(2,128)S(1)} %pad_maximum_fusion.2), channel_id=1, replica_groups=mesh['data'=32] {'data'}, use_global_device_ids=true, to_apply=%region_5.6 | all-reduce | flops 8192 | bytes 65536 | tf_op jit(solution)/shard_map/psum | solution.py:14
  124.6 15.8 %fusion.34 = (f32[2,2048]{1,0:T(2,128)S(1)}, f32[2,2048]{1,0:T(2,128)S(1)}, f32[2,512,2048]{2,1,0:T(8,128)}) fusion(bf16[2048,2048]{1,0:T(8,128)(2,1)} %param.14, f32[2,512,2048]{2,1,0:T(8,128)} %get-tuple-element.31, f32[2048]{0:T(1024)S(1)} %copy-done.8, f32[2,2048]{1,0:T(2,128)S(1)} %fusion.25, f32[2,2048]{1,0:T(2,128)S(1)} %fusion.26, ...), kind=kOutput, calls=%fused_computation.83 | convolution fusion | flops 8608800768 | bytes 25247744 | tf_op jit(solution)/shard_map/dot_general | solution.py:41
  140.4 39.8 %psum.51 = f32[2,2,2048]{2,1,0:T(2,128)S(1)} all-reduce(f32[2,2,2048]{2,1,0:T(2,128)S(1)} %pad_maximum_fusion.3), channel_id=1, replica_groups=mesh['data'=32] {'data'}, use_global_device_ids=true, to_apply=%region_8.9 | all-reduce | flops 8192 | bytes 65536 | tf_op jit(solution)/shard_map/psum | solution.py:14
  180.3 4.6 fusion.10
  185.0 1.9 copy-done.3
  186.9 8.1 fusion.16
  195.0 0.0 all-reduce.2.cloned.1.call-update
  195.0 0.2 reduce-scatter.8.cloned.1.call-start
  195.9 277.2 %all-reduce.2.cloned.1.call-done = f32[2048,2048]{1,0:T(8,128)} async-done(((f32[2048,2048]{1,0:T(8,128)}), f32[2048,2048]{1,0:T(8,128)}) %all-reduce.2.cloned.1.call-update) | async-done | bytes 16777232 | tf_op jit(solution)/shard_map/psum | solution.py:45
  473.1 12.4 %convolution_bitcast_fusion.3 = f32[1,512,2048]{2,1,0:T(8,128)} fusion(bf16[2,512,2048]{2,1,0:T(8,128)(2,1)} %copy-done.3, f32[2048,2048]{1,0:T(8,128)} %all-reduce.2.cloned.1.call-done, f32[]{:T(128)S(6)} %mul.190), kind=kOutput, calls=%fused_computation.38 | convolution fusion | flops 4328521728 | bytes 23068676 | tf_op jit(solution)/shard_map/dot_general | solution.py:52
  485.5 9.3 convolution_bitcast_fusion.2
  494.7 0.0 slice-done.1
  494.7 4.6 fusion.11
  499.3 40.6 %psum.53 = f32[2,2,2048]{2,1,0:T(2,128)S(1)} all-reduce(f32[2,2,2048]{2,1,0:T(2,128)S(1)} %pad_maximum_fusion.4), channel_id=1, replica_groups=mesh['data'=32] {'data'}, use_global_device_ids=true, to_apply=%region_13.14 | all-reduce | flops 8192 | bytes 65536 | tf_op jit(solution)/shard_map/psum | solution.py:21
  539.9 7.1 multiply_convert_fusion.3
  547.0 1.9 copy-done.1
  548.9 14.8 %convolution_bitcast_fusion = f32[2048,2048]{1,0:T(8,128)} fusion(bf16[2,512,2048]{2,1,0:T(8,128)(2,1)S(1)} %multiply_convert_fusion.3, f32[2,512,2048]{2,1,0:T(8,128)} %get-tuple-element.31, f32[2048]{0:T(1024)S(1)} %copy-done.8, f32[2,2048]{1,0:T(2,128)S(1)} %fusion.25, f32[2,2048]{1,0:T(2,128)S(1)} %fusion.26, f32[2048]{0:T(1024)S(1)} %copy-done.6), kind=kOutput, calls=%fused_computation.3 | convolution fusion | flops 8602517504 | bytes 29409280 | tf_op jit(solution)/shard_map/dot_general | solution.py:58
  563.7 0.0 reduce-scatter.8.cloned.1.call-update
  563.7 0.0 reduce-scatter.6.cloned.1.call-start
  563.8 16.9 %fusion.33 = (f32[2,2048]{1,0:T(2,128)S(1)}, f32[2,2048]{1,0:T(2,128)S(1)}, f32[2,512,2048]{2,1,0:T(8,128)}) fusion(f32[2,2048]{1,0:T(2,128)S(1)} %fusion.25, f32[2,512,2048]{2,1,0:T(8,128)} %get-tuple-element.31, f32[2,2048]{1,0:T(2,128)S(1)} %fusion.26, bf16[2,512,2048]{2,1,0:T(8,128)(2,1)} %copy-done.1, bf16[2048,2048]{1,0:T(8,128)(2,1)} %param.14, ...), kind=kOutput, calls=%fused_computation.82 | convolution fusion | flops 8608800768 | bytes 29442048 | tf_op jit(solution)/shard_map/dot_general | solution.py:60
  580.7 43.0 %psum.54 = f32[2,2,2048]{2,1,0:T(2,128)S(1)} all-reduce(f32[2,2,2048]{2,1,0:T(2,128)S(1)} %pad_maximum_fusion.5), channel_id=1, replica_groups=mesh['data'=32] {'data'}, use_global_device_ids=true, to_apply=%region_16.17 | all-reduce | flops 8192 | bytes 65536 | tf_op jit(solution)/shard_map/psum | solution.py:21
  623.8 0.6 slice_reduce_fusion.3
  624.4 7.1 multiply_convert_fusion.2
  631.6 1.9 copy-done.2
  633.5 14.8 %convolution_bitcast_fusion.1 = f32[2048,2048]{1,0:T(8,128)} fusion(bf16[2,512,2048]{2,1,0:T(8,128)(2,1)S(1)} %multiply_convert_fusion.2, f32[1024,2048]{1,0:T(8,128)} %get-tuple-element.30, f32[2048]{0:T(1024)S(1)} %copy-done.9, f32[2,2048]{1,0:T(2,128)S(1)} %fusion.30, f32[2,2048]{1,0:T(2,128)S(1)} %fusion.31, f32[2048]{0:T(1024)S(1)} %copy-done.7), kind=kOutput, calls=%fused_computation.4 | convolution fusion | flops 8602517504 | bytes 29409280 | tf_op jit(solution)/shard_map/dot_general | solution.py:65
  648.3 0.0 reduce-scatter.6.cloned.1.call-update
  648.3 0.0 reduce-scatter.4.cloned.1.call-start
  648.3 16.9 %fusion.32 = (f32[2,2048]{1,0:T(2,128)S(1)}, f32[2,2048]{1,0:T(2,128)S(1)}, f32[2,512,2048]{2,1,0:T(8,128)}) fusion(f32[2,2048]{1,0:T(2,128)S(1)} %fusion.30, f32[2,2048]{1,0:T(2,128)S(1)} %fusion.31, f32[1024,2048]{1,0:T(8,128)} %get-tuple-element.30, bf16[2,512,2048]{2,1,0:T(8,128)(2,1)} %copy-done.2, bf16[2048,2048]{1,0:T(8,128)(2,1)} %param.13, ...), kind=kOutput, calls=%fused_computation.81 | convolution fusion | flops 8608800768 | bytes 29442048 | tf_op jit(solution)/shard_map/dot_general | solution.py:67
  665.3 44.1 %psum.55 = f32[2,2,2048]{2,1,0:T(2,128)S(1)} all-reduce(f32[2,2,2048]{2,1,0:T(2,128)S(1)} %pad_maximum_fusion.6), channel_id=1, replica_groups=mesh['data'=32] {'data'}, use_global_device_ids=true, to_apply=%region_19.20 | all-reduce | flops 8192 | bytes 65536 | tf_op jit(solution)/shard_map/psum | solution.py:21
  709.4 0.6 slice_reduce_fusion.1
  710.1 7.2 multiply_convert_fusion.1
  717.3 11.7 %fusion.36 = f32[2048,2048]{1,0:T(8,128)} fusion(bf16[1024,2048]{1,0:T(8,128)(2,1)S(1)} %copy-done.5, bf16[1024,2048]{1,0:T(8,128)(2,1)S(1)} %bitcast.129), kind=kOutput, calls=%fused_computation.85 | convolution fusion | flops 8589934592 | bytes 25165824 | tf_op jit(solution)/shard_map/dot_general | solution.py:72
  729.1 0.0 reduce-scatter.4.cloned.1.call-update
  729.1 8.8 select_reduce_fusion
  737.8 10.9 reduce-scatter.8.cloned.1.call-done
  748.7 187.4 %reduce-scatter.6.cloned.1.call-done = f32[64,2048]{1,0:T(8,128)} async-done(((f32[2048,2048]{1,0:T(8,128)}), f32[64,2048]{1,0:T(8,128)}) %reduce-scatter.6.cloned.1.call-update) | async-done | bytes 524304 | tf_op jit(solution)/shard_map/reduce_scatter | solution.py:64
  936.1 187.3 %reduce-scatter.4.cloned.1.call-done = f32[64,2048]{1,0:T(8,128)} async-done(((f32[2048,2048]{1,0:T(8,128)}), f32[64,2048]{1,0:T(8,128)}) %reduce-scatter.4.cloned.1.call-update) | async-done | bytes 524304 | tf_op jit(solution)/shard_map/reduce_scatter | solution.py:71
  (29 shorter events, 0.2 us)
Async XLA Ops:
  7.2 465.9 %all-reduce.2.cloned.1.call-start = ((), (), s32[]{:S(2)}) async-start(), calls=%async_computation.3 | async-start | bytes 33554432 | tf_op jit(solution)/shard_map/psum | solution.py:45
  10.7 14.8 %copy-start.4 = (bf16[1024,2048]{1,0:T(8,128)(2,1)}, bf16[1024,2048]{1,0:T(8,128)(2,1)S(1)}, u32[]{:S(2)}) copy-start(bf16[1024,2048]{1,0:T(8,128)(2,1)S(1)} %constant_dynamic-update-slice_fusion) | copy-start | bytes 12582916
  10.7 57.0 %copy-start.7 = (f32[2048]{0:T(1024)S(1)}, f32[2048]{0:T(1024)}, u32[]{:S(2)}) copy-start(f32[2048]{0:T(1024)} %param.15) | copy-start | bytes 24580
  10.7 57.0 %copy-start.9 = (f32[2048]{0:T(1024)S(1)}, f32[2048]{0:T(1024)}, u32[]{:S(2)}) copy-start(f32[2048]{0:T(1024)} %param.16) | copy-start | bytes 24580
  67.7 56.9 %copy-start.6 = (f32[2048]{0:T(1024)S(1)}, f32[2048]{0:T(1024)}, u32[]{:S(2)}) copy-start(f32[2048]{0:T(1024)} %param.17) | copy-start | bytes 24580
  67.7 56.9 %copy-start.8 = (f32[2048]{0:T(1024)S(1)}, f32[2048]{0:T(1024)}, u32[]{:S(2)}) copy-start(f32[2048]{0:T(1024)} %param.18) | copy-start | bytes 24580
  185.0 1.9 copy-start.3
  195.0 553.7 %reduce-scatter.8.cloned.1.call-start = ((), (), s32[]{:S(2)}) async-start(), calls=%async_computation.6 | async-start | bytes 17301504 | tf_op jit(solution)/shard_map/reduce_scatter | solution.py:57
  473.0 12.4 %copy-start = (f32[2048,2048]{1,0:T(8,128)S(1)}, f32[2048,2048]{1,0:T(8,128)}, u32[]{:S(2)}) copy-start(f32[2048,2048]{1,0:T(8,128)} %all-reduce.2.cloned.1.call-done) | copy-start | bytes 50331652
  473.0 21.7 %slice-start = ((s8[8388608]{0:T(1024)(128)(4,1)}), s8[4194304]{0:T(1024)(128)(4,1)S(1)}, s32[]{:S(2)}) async-start(s8[8388608]{0:T(1024)(128)(4,1)} %bitcast.127), calls=%async_computation.7 | async-start | bytes 8388608
  485.5 9.3 slice-start.1
  547.0 1.9 copy-start.1
  563.7 372.4 %reduce-scatter.6.cloned.1.call-start = ((), (), s32[]{:S(2)}) async-start(), calls=%async_computation.5 | async-start | bytes 17301504 | tf_op jit(solution)/shard_map/reduce_scatter | solution.py:64
  631.5 1.9 copy-start.2
  648.3 475.1 %reduce-scatter.4.cloned.1.call-start = ((), (), s32[]{:S(2)}) async-start(), calls=%async_computation.4 | async-start | bytes 17301504 | tf_op jit(solution)/shard_map/reduce_scatter | solution.py:71
  710.1 7.2 copy-start.5
Sparse Core Ops, SparseCore 0:
  195.1 277.8 all-reduce.1
  563.9 184.7 reduce-scatter.7
  751.6 184.5 reduce-scatter.5
  938.8 184.5 reduce-scatter.3
where the time goes:
time: 1140 us; the launch traced here: 1130 us
  waiting for transfers between devices  663 us (58%)
  blocking collectives  251 us (22%)
  matrix products  151 us (13%)
  other arithmetic  40.9 us (4%)
  between operations  15.2 us (1%)
    psum x1, waiting for transfers between devices, local_step(): corr_mat = lax.psum(corr_part, 'data') / total_rows  277 us
    reduce_scatter x1, waiting for transfers between devices, local_step(): lax.psum_scatter(lax.dot_general(act_one, grad_hidden_two, ROW_DIMS, pref...  187 us
    reduce_scatter x1, waiting for transfers between devices, local_step(): lax.psum_scatter(lax.dot_general(feat_rows, grad_hidden_one, FIRST_DIMS,...  187 us
    psum x3, blocking collectives, norm_backward(): lax.psum(jnp.stack([jnp.sum(grad_out, axis=1), jnp.sum(grad_out * normed,...  128 us
    psum x3, blocking collectives, norm_forward(): col_sums = lax.psum(col_sums, 'data')  123 us
  transfers between devices with their start and end apart: 4, of which 4 were waited for; matrix products, arithmetic and copies ran while one was open for 8% of the time, Pallas kernels for 0%

commit v1 on v0

v1 whole, which is shorter than its diff:
```python
import functools

import jax
import jax.numpy as jnp
from jax import lax
from jax.experimental import pallas as pl
from jax.experimental.pallas import tpu as pltpu
from jax.sharding import PartitionSpec as P

NORM_EPS = 1e-5
ROW_DIMS = (((0, 1), (0, 1)), ((), ()))
FIRST_DIMS = (((0,), (0,)), ((), ()))
LAST_DIMS = (((2,), (1,)), ((), ()))
MESH = pl.DeviceIdType.MESH
F32 = jnp.float32
BF16 = jnp.bfloat16


class Place:
    def __init__(self):
        me = lax.axis_index("data")
        self.core = lax.rem(me, 2)
        self.x = lax.rem(lax.div(me, 2), 2)
        self.y = lax.rem(lax.div(me, 4), 2)
        self.z = lax.div(me, 8)
        self.plane = lax.rem(lax.div(me, 2), 4)
        self.partner = me + 1 - 2 * self.core
        self.x_peer = me + 2 - 4 * self.x
        self.y_peer = me + 4 - 8 * self.y
        low = lax.rem(me, 8)
        self.z_peers = [lax.rem(self.z + d, 4) * 8 + low for d in (1, 2, 3)]
        self.plane_peers = [
            self.z * 8 + lax.rem(self.plane + d, 4) * 2 + self.core for d in (1, 2, 3)
        ]


def enter(peers):
    barrier = pltpu.get_barrier_semaphore()
    for peer in peers:
        pl.semaphore_signal(barrier, inc=1, device_id=(peer,), device_id_type=MESH)
    pl.semaphore_wait(barrier, len(peers))


def remote(src, dst, send_sem, recv_sem, peer):
    return pltpu.make_async_remote_copy(
        src_ref=src, dst_ref=dst, send_sem=send_sem, recv_sem=recv_sem,
        device_id=(peer,), device_id_type=MESH)


def sums_kernel(in_ref, out_ref, recv0, slots1, slots2, send_sem, recv_sem):
    at = Place()
    half = in_ref.shape[1] // 2
    enter([at.partner] + at.plane_peers + at.z_peers)
    mine = pl.ds(pl.multiple_of(at.core * half, 128), half)
    theirs = pl.ds(pl.multiple_of((1 - at.core) * half, 128), half)
    first = remote(in_ref.at[:, theirs], recv0, send_sem.at[0], recv_sem.at[0], at.partner)
    first.start()
    first.wait()
    slots1[at.plane] = in_ref[:, mine] + recv0[...]
    copies = []
    for d in range(3):
        copies.append(remote(slots1.at[at.plane], slots1.at[at.plane], send_sem.at[1 + d], recv_sem.at[1 + d],
                             at.plane_peers[d]))
        copies[-1].start()
    for copy in copies:
        copy.wait()
    slots2[at.z] = (slots1[0] + slots1[1]) + (slots1[2] + slots1[3])
    copies = []
    for d in range(3):
        copies.append(remote(slots2.at[at.z], slots2.at[at.z], send_sem.at[4 + d], recv_sem.at[4 + d],
                             at.z_peers[d]))
        copies[-1].start()
    for copy in copies:
        copy.wait()
    out_ref[:, mine] = (slots2[0] + slots2[1]) + (slots2[2] + slots2[3])
    last = remote(out_ref.at[:, mine], out_ref.at[:, mine], send_sem.at[7], recv_sem.at[7], at.partner)
    last.start()
    last.wait()


def all_sums(values, collective_id):
    rows, cols = values.shape
    return pl.pallas_call(
        sums_kernel,
        out_shape=jax.ShapeDtypeStruct(values.shape, F32),
        in_specs=[pl.BlockSpec(memory_space=pltpu.VMEM)],
        out_specs=pl.BlockSpec(memory_space=pltpu.VMEM),
        scratch_shapes=[
            pltpu.VMEM((rows, cols // 2), F32),
            pltpu.VMEM((4, rows, cols // 2), F32),
            pltpu.VMEM((4, rows, cols // 2), F32),
            pltpu.SemaphoreType.DMA((8,)),
            pltpu.SemaphoreType.DMA((8,)),
        ],
        compiler_params=pltpu.CompilerParams(collective_id=collective_id, has_side_effects=True),
    )(values)


class Scatter:
    def __init__(self, at, part, bufs, send_sem, recv_sem, chunk):
        self.at, self.part, self.chunk = at, part, chunk
        self.recv0, self.snd1, self.recv1, self.snd2, self.recv2, self.snd3, self.recv3 = bufs
        self.send_sem, self.recv_sem = send_sem, recv_sem
        self.copies = {}

    def cols(self, j):
        return pl.ds(j * self.chunk, self.chunk)

    def start(self, j, stage, src, dst, peer):
        copy = remote(src, dst, self.send_sem.at[j, stage], self.recv_sem.at[j, stage], peer)
        copy.start()
        self.copies[j, stage] = copy

    def total(self, j, z, y, x, depth):
        cs, c = self.cols(j), self.at.core
        total = self.part[z, y, x, c, :, cs].astype(F32) + self.recv0[z, y, x, :, cs].astype(F32)
        if depth > 1:
            total += self.recv1[z, y if j % 2 == 0 else x, :, cs].astype(F32)
        if depth > 2:
            total += self.recv2[z, :, cs].astype(F32)
        return total

    def stage0(self, j):
        cs, at = self.cols(j), self.at
        self.start(j, 0, self.part.at[:, :, :, 1 - at.core, :, cs], self.recv0.at[:, :, :, :, cs], at.partner)

    def stage1(self, j):
        cs, at = self.cols(j), self.at
        self.copies[j, 0].wait()
        for z in range(4):
            for k in range(2):
                y, x = (k, 1 - at.x) if j % 2 == 0 else (1 - at.y, k)
                self.snd1[z, k, :, cs] = self.total(j, z, y, x, 1).astype(BF16)
        self.start(j, 1, self.snd1.at[:, :, :, cs], self.recv1.at[:, :, :, cs], at.x_peer if j % 2 == 0 else at.y_peer)

    def stage2(self, j):
        cs, at = self.cols(j), self.at
        self.copies[j, 1].wait()
        for z in range(4):
            y, x = (1 - at.y, at.x) if j % 2 == 0 else (at.y, 1 - at.x)
            self.snd2[z, :, cs] = self.total(j, z, y, x, 2).astype(BF16)
        self.start(j, 2, self.snd2.at[:, :, cs], self.recv2.at[:, :, cs], at.y_peer if j % 2 == 0 else at.x_peer)

    def stage3(self, j):
        cs, at = self.cols(j), self.at
        self.copies[j, 2].wait()
        for d in range(3):
            z = lax.rem(at.z + d + 1, 4)
            self.snd3[d, :, cs] = self.total(j, z, at.y, at.x, 3).astype(BF16)
            self.start(j, 3 + d, self.snd3.at[d, :, cs], self.recv3.at[d, :, cs], at.z_peers[d])

    def final(self, j):
        cs, at = self.cols(j), self.at
        total = self.total(j, at.z, at.y, at.x, 3)
        for d in range(3):
            self.copies[j, 3 + d].wait()
            total += self.recv3[d, :, cs].astype(F32)
        return total


def scatter_scratch(rows, cols, chunks, stages):
    return [
        pltpu.VMEM((4, 2, 2, rows, cols), BF16),
        pltpu.VMEM((4, 2, rows, cols), BF16),
        pltpu.VMEM((4, 2, rows, cols), BF16),
        pltpu.VMEM((4, rows, cols), BF16),
        pltpu.VMEM((4, rows, cols), BF16),
        pltpu.VMEM((3, rows, cols), BF16),
        pltpu.VMEM((3, rows, cols), BF16),
        pltpu.SemaphoreType.DMA((chunks, stages)),
        pltpu.SemaphoreType.DMA((chunks, stages)),
    ]


def scatter_kernel(chunks, part_ref, out_ref, *scratch):
    at = Place()
    enter([at.partner, at.x_peer, at.y_peer] + at.z_peers)
    send_sem, recv_sem = scratch[7:]
    chunk = part_ref.shape[-1] // chunks
    scatter = Scatter(at, part_ref, scratch[:7], send_sem, recv_sem, chunk)
    for j in range(chunks):
        scatter.stage0(j)
    for t in range(chunks + 3):
        for stage, step in enumerate((scatter.stage1, scatter.stage2, scatter.stage3)):
            if 0 <= t - stage < chunks:
                step(t - stage)
        j = t - 3
        if j >= 0:
            out_ref[:, scatter.cols(j)] = scatter.final(j)


def scatter_sum(part, collective_id, chunks=8):
    full, cols = part.shape
    rows = full // 32
    return pl.pallas_call(
        functools.partial(scatter_kernel, chunks),
        out_shape=jax.ShapeDtypeStruct((rows, cols), F32),
        in_specs=[pl.BlockSpec(memory_space=pltpu.VMEM)],
        out_specs=pl.BlockSpec(memory_space=pltpu.VMEM),
        scratch_shapes=scatter_scratch(rows, cols, chunks, 6),
        compiler_params=pltpu.CompilerParams(
            collective_id=collective_id, has_side_effects=True, vmem_limit_bytes=40 * 2**20),
    )(part.reshape(4, 2, 2, 2, rows, cols))


def corr_kernel(chunks, total_rows, part_ref, lam_ref, grad_ref, loss_ref, *scratch):
    at = Place()
    enter([at.partner, at.x_peer, at.y_peer] + at.z_peers)
    send_sem, recv_sem = scratch[7:]
    rows, cols = part_ref.shape[-2:]
    chunk = cols // chunks
    scatter = Scatter(at, part_ref, scratch[:7], send_sem, recv_sem, chunk)
    lam = lam_ref[0]
    block = grad_ref.at[at.z, at.y, at.x, at.core]
    first_row = (((at.z * 2 + at.y) * 2 + at.x) * 2 + at.core) * rows

    def spread_z(j):
        cs = scatter.cols(j)
        corr = scatter.final(j) / total_rows
        row = first_row + lax.broadcasted_iota(jnp.int32, corr.shape, 0)
        col = j * chunk + lax.broadcasted_iota(jnp.int32, corr.shape, 1)
        diag = row == col
        gap = 1.0 - corr
        loss_ref[:, cs] = jnp.sum(jnp.where(diag, gap * gap, lam * corr * corr), axis=0, keepdims=True)
        grad = jnp.where(diag, -2.0 * gap, 2.0 * lam * corr)
        block[:, cs] = (grad / total_rows).astype(BF16)
        for d in range(3):
            scatter.start(j, 6 + d, block.at[:, cs], block.at[:, cs], at.z_peers[d])

    def spread_one(j):
        cs = scatter.cols(j)
        for d in range(3):
            scatter.copies[j, 6 + d].wait()
        here = grad_ref.at[:, at.y, at.x, at.core, :, cs]
        scatter.start(j, 9, here, here, at.y_peer if j % 2 == 0 else at.x_peer)

    def spread_two(j):
        cs = scatter.cols(j)
        scatter.copies[j, 9].wait()
        if j % 2 == 0:
            here, peer = grad_ref.at[:, :, at.x, at.core, :, cs], at.x_peer
        else:
            here, peer = grad_ref.at[:, at.y, :, at.core, :, cs], at.y_peer
        scatter.start(j, 10, here, here, peer)

    def spread_core(j):
        cs = scatter.cols(j)
        scatter.copies[j, 10].wait()
        here = grad_ref.at[:, :, :, at.core, :, cs]
        scatter.start(j, 11, here, here, at.partner)

    def finish(j):
        scatter.copies[j, 11].wait()

    steps = (scatter.stage1, scatter.stage2, scatter.stage3, spread_z, spread_one, spread_two, spread_core, finish)
    for j in range(chunks):
        scatter.stage0(j)
    for t in range(chunks + len(steps) - 1):
        for stage, step in enumerate(steps):
            if 0 <= t - stage < chunks:
                step(t - stage)


def corr_grad(part, lam, total_rows, collective_id, chunks=8):
    full, cols = part.shape
    rows = full // 32
    grad, loss = pl.pallas_call(
        functools.partial(corr_kernel, chunks, total_rows),
        out_shape=(jax.ShapeDtypeStruct((4, 2, 2, 2, rows, cols), BF16), jax.ShapeDtypeStruct((1, cols), F32)),
        in_specs=[pl.BlockSpec(memory_space=pltpu.VMEM), pl.BlockSpec(memory_space=pltpu.SMEM)],
        out_specs=(pl.BlockSpec(memory_space=pltpu.VMEM), pl.BlockSpec(memory_space=pltpu.VMEM)),
        scratch_shapes=scatter_scratch(rows, cols, chunks, 12),
        compiler_params=pltpu.CompilerParams(
            collective_id=collective_id, has_side_effects=True, vmem_limit_bytes=48 * 2**20),
    )(part.reshape(4, 2, 2, 2, rows, cols), lam.reshape(1))
    return grad.reshape(full, cols), loss


def norm_forward(values, total_rows, collective_id):
    cols = values.shape[-1]
    col_sums = jnp.concatenate([jnp.sum(values, axis=1), jnp.sum(values * values, axis=1)])
    col_sums = all_sums(col_sums, collective_id).reshape(2, 2, cols)
    col_mean = col_sums[0] / total_rows
    inv_std = lax.rsqrt(col_sums[1] / total_rows - col_mean * col_mean + NORM_EPS)
    return (values - col_mean[:, None, :]) * inv_std[:, None, :], inv_std


def norm_backward(grad_out, normed, inv_std, total_rows, collective_id, extra=None):
    cols = grad_out.shape[-1]
    rows = [jnp.sum(grad_out, axis=1), jnp.sum(grad_out * normed, axis=1)]
    if extra is not None:
        rows.append(extra)
    summed = all_sums(jnp.concatenate(rows), collective_id)
    col_sums = summed[:4].reshape(2, 2, cols)
    grad_in = inv_std[:, None, :] * (grad_out - (col_sums[0][:, None, :] + normed * col_sums[1][:, None, :]) / total_rows)
    return grad_in, col_sums, summed[4:]


def solution(mesh):
    shards = mesh.shape["data"]

    def local_step(h_a, h_b, w_one, w_two, w_three, gain_one, shift_one, gain_two, shift_two, lam_off):
        rows_dev = h_a.shape[0]
        total_rows = rows_dev * shards
        feat_rows = jnp.concatenate([h_a, h_b], axis=0)
        hidden_one = jnp.dot(feat_rows, w_one, preferred_element_type=F32).reshape(2, rows_dev, -1)
        normed_one, inv_one = norm_forward(hidden_one, total_rows, 0)
        pre_one = gain_one * normed_one + shift_one
        act_one = jax.nn.relu(pre_one).astype(BF16)
        hidden_two = jnp.dot(act_one, w_two, preferred_element_type=F32)
        normed_two, inv_two = norm_forward(hidden_two, total_rows, 1)
        pre_two = gain_two * normed_two + shift_two
        act_two = jax.nn.relu(pre_two).astype(BF16)
        proj_out = jnp.dot(act_two, w_three, preferred_element_type=F32)
        normed_out, inv_out = norm_forward(proj_out, total_rows, 2)
        embed_pair = normed_out.astype(BF16)
        corr_part = lax.dot_general(embed_pair[0], embed_pair[1], FIRST_DIMS, preferred_element_type=F32)
        grad_scaled, loss_cols = corr_grad(corr_part.astype(BF16), lam_off, total_rows, 3)
        grad_embed_a = lax.dot_general(embed_pair[1], grad_scaled, (((1,), (1,)), ((), ())),
                                       preferred_element_type=F32)
        grad_embed_b = jnp.dot(embed_pair[0], grad_scaled, preferred_element_type=F32)
        grad_embed = jnp.stack([grad_embed_a, grad_embed_b])
        grad_proj, _, loss_cols = norm_backward(grad_embed, normed_out, inv_out, total_rows, 4, loss_cols)
        loss_total = jnp.sum(loss_cols)
        grad_proj = grad_proj.astype(BF16)
        grad_w_three = scatter_sum(
            lax.dot_general(act_two, grad_proj, ROW_DIMS, preferred_element_type=F32).astype(BF16), 5)
        grad_act_two = lax.dot_general(grad_proj, w_three, LAST_DIMS, preferred_element_type=F32)
        grad_pre_two = jnp.where(pre_two > 0, grad_act_two, 0.0)
        grad_hidden_two, sums_two, _ = norm_backward(grad_pre_two, normed_two, inv_two, total_rows, 6)
        grad_hidden_two = (gain_two * grad_hidden_two).astype(BF16)
        grad_w_two = scatter_sum(
            lax.dot_general(act_one, grad_hidden_two, ROW_DIMS, preferred_element_type=F32).astype(BF16), 7)
        grad_act_one = lax.dot_general(grad_hidden_two, w_two, LAST_DIMS, preferred_element_type=F32)
        grad_pre_one = jnp.where(pre_one > 0, grad_act_one, 0.0)
        grad_hidden_one, sums_one, _ = norm_backward(grad_pre_one, normed_one, inv_one, total_rows, 8)
        grad_hidden_one = (gain_one * grad_hidden_one).astype(BF16).reshape(2 * rows_dev, -1)
        grad_w_one = scatter_sum(
            lax.dot_general(feat_rows, grad_hidden_one, FIRST_DIMS, preferred_element_type=F32).astype(BF16), 9)
        return (loss_total, grad_w_one, grad_w_two, grad_w_three,
                jnp.sum(sums_one[1], axis=0), jnp.sum(sums_one[0], axis=0),
                jnp.sum(sums_two[1], axis=0), jnp.sum(sums_two[0], axis=0))

    row_spec = P("data", None)
    whole_mat = P(None, None)
    whole_vec = P(None)
    return jax.shard_map(
        local_step, mesh=mesh,
        in_specs=(row_spec, row_spec, whole_mat, whole_mat, whole_mat,
                  whole_vec, whole_vec, whole_vec, whole_vec, P()),
        out_specs=(P(), row_spec, row_spec, row_spec, whole_vec, whole_vec, whole_vec, whole_vec),
        check_vma=False)
```

time: 1140 us -> 531 us (0.47)
  waiting for transfers between devices: 663 us -> 0 us
  Pallas kernels: 0 us -> 336 us
  blocking collectives: 251 us -> 0 us
  matrix products: 151 us -> 134 us
  between operations: 15.2 us -> 1.9 us
    reduce_scatter x3 -> x0, waiting for transfers between devices: 386 us -> none  [the longest x1 187 us: local_step(): lax.psum_scatter(lax.dot_general(act_one, grad_hidden_two, ROW_DIMS, pref...]
    pallas_call x0 -> x10, Pallas kernels: none -> 336 us  [the longest x3 155 us: scatter_sum(): pl.pallas_call(functools.partial(scatter_kernel, chunks), out_shape=jax.S...]
    psum x1 -> x0, waiting for transfers between devices: 277 us -> none  [local_step(): corr_mat = lax.psum(corr_part, 'data') / total_rows]
    psum x6 -> x0, blocking collectives: 251 us -> none  [the longest x3 128 us: norm_backward(): lax.psum(jnp.stack([jnp.sum(grad_out, axis=1), jnp.sum(grad_out * normed,...]
  transfers between devices with their start and end apart: 4 -> 0, of which waited for: 4 -> 0; matrix products, arithmetic and copies ran while one was open for 8% -> 0% of each run, Pallas kernels for 0% -> 0%
where the time goes in v1:
time: 531 us; the launch traced here: 521 us
  Pallas kernels  336 us (63%)
  matrix products  134 us (25%)
  other arithmetic  41.1 us (8%)
  local copies, waits for them, and re-layouts  8 us (2%)
    pallas_call x3, Pallas kernels, scatter_sum(): pl.pallas_call(functools.partial(scatter_kernel, chunks), out_shape=jax.S...  155 us
    pallas_call x1, Pallas kernels, corr_grad(): pl.pallas_call(functools.partial(corr_kernel, chunks, total_rows), out_sh...  96.9 us
    pallas_call x6, Pallas kernels, all_sums(): pl.pallas_call(sums_kernel, out_shape=jax.ShapeDtypeStruct(values.shape,...  84.7 us
    dot_general x1, matrix products, local_step(): lax.dot_general(grad_proj, w_three, LAST_DIMS, preferred_element_type=F32)  16.2 us
    dot_general x1, matrix products, local_step(): proj_out = jnp.dot(act_two, w_three, preferred_element_type=F32)  15.9 us
    dot_general x1, matrix products, local_step(): hidden_two = jnp.dot(act_one, w_two, preferred_element_type=F32)  15.8 us
    dot_general x1, matrix products, local_step(): lax.dot_general(grad_hidden_two, w_two, LAST_DIMS, preferred_element_type...  15.8 us
    dot_general x1, matrix products, local_step(): lax.dot_general(act_two, grad_proj, ROW_DIMS, preferred_element_type=F32)  13.3 us

profile of v1, /device:TPU:0, one launch (start us, length us, event | category | flops | bytes accessed | tf_op | source)
XLA Modules:
  0.0 521.2 jit_solution(12634798219771764719)
XLA Ops:
  1.3 1.9 constant_dynamic-update-slice_fusion.1
  3.2 2.0 constant_dynamic-update-slice_fusion
  5.2 0.7 copy-done.8
  5.9 11.0 %bitcast_reduce_fusion = (f32[2,2048]{1,0:T(2,128)S(1)}, f32[2,2048]{1,0:T(2,128)S(1)}, f32[1024,2048]{1,0:T(8,128)}) fusion(bf16[1024,2048]{1,0:T(8,128)(2,1)S(1)} %constant_dynamic-update-slice_fusion, bf16[2048,2048]{1,0:T(8,128)(2,1)S(1)} %copy-done.8), kind=kOutput, calls=%fused_computation.13 | convolution fusion | flops 8596217856 | bytes 21004288 | tf_op jit(solution)/shard_map/dot_general | solution.py:306
  17.0 0.6 pad_maximum_fusion.2.in_ref
  17.6 15.1 %shard_map.161 = f32[4,2048]{1,0:T(4,128)} custom-call(f32[4,2048]{1,0:T(4,128)} %pad_maximum_fusion.2.in_ref), custom_call_target="tpu_custom_call" | custom-call | tf_op jit(solution)/shard_map/pallas_call | solution.py:83
  32.7 0.9 slice_multiply_fusion.2
  33.6 0.0 copy-start.6
  33.6 0.0 copy-start.9
  33.6 15.8 %fusion.19 = (f32[2,2048]{1,0:T(2,128)S(1)}, f32[2,2048]{1,0:T(2,128)S(1)}, f32[2,512,2048]{2,1,0:T(8,128)}) fusion(bf16[2048,2048]{1,0:T(8,128)(2,1)} %param.13, f32[1024,2048]{1,0:T(8,128)} %get-tuple-element.40, f32[2048]{0:T(1024)S(1)} %copy-done.10, f32[2,2048]{1,0:T(2,128)S(1)} %get-tuple-element.39, f32[2,2048]{1,0:T(2,128)S(1)} %get-tuple-element.38, ...), kind=kOutput, calls=%fused_computation.62 | convolution fusion | flops 8608800768 | bytes 25247744 | tf_op jit(solution)/shard_map/dot_general | solution.py:310
  49.4 0.6 pad_maximum_fusion.3.in_ref
  50.1 12.8 %shard_map.162 = f32[4,2048]{1,0:T(4,128)} custom-call(f32[4,2048]{1,0:T(4,128)} %pad_maximum_fusion.3.in_ref), custom_call_target="tpu_custom_call" | custom-call | tf_op jit(solution)/shard_map/pallas_call | solution.py:83
  62.9 0.9 slice_multiply_fusion.1
  63.8 15.9 %fusion.18 = (f32[2,2048]{1,0:T(2,128)S(1)}, f32[2,2048]{1,0:T(2,128)S(1)}, f32[2,512,2048]{2,1,0:T(8,128)}) fusion(bf16[2048,2048]{1,0:T(8,128)(2,1)} %param.14, f32[2,512,2048]{2,1,0:T(8,128)} %get-tuple-element.41, f32[2048]{0:T(1024)S(1)} %copy-done.9, f32[2,2048]{1,0:T(2,128)S(1)} %get-tuple-element.37, f32[2,2048]{1,0:T(2,128)S(1)} %get-tuple-element.36, ...), kind=kOutput, calls=%fused_computation.61 | convolution fusion | flops 8608800768 | bytes 25247744 | tf_op jit(solution)/shard_map/dot_general | solution.py:314
  79.7 0.6 pad_maximum_fusion.4.in_ref
  80.4 11.9 %shard_map.163 = f32[4,2048]{1,0:T(4,128)} custom-call(f32[4,2048]{1,0:T(4,128)} %pad_maximum_fusion.4.in_ref), custom_call_target="tpu_custom_call" | custom-call | tf_op jit(solution)/shard_map/pallas_call | solution.py:83
  92.3 0.9 slice_multiply_fusion
  93.1 4.6 fusion.10
  97.8 6.9 %convolution_convert_fusion.1 = bf16[2048,2048]{1,0:T(8,128)(2,1)} fusion(bf16[2,512,2048]{2,1,0:T(8,128)(2,1)S(1)} %fusion.10), kind=kOutput, calls=%fused_computation.33 | convolution fusion | flops 4299161600 | bytes 12582912 | tf_op jit(solution)/shard_map/dot_general | solution.py:317
  104.6 96.9 %shard_map.164 = (bf16[4,2,2,2,64,2048]{5,4,3,2,1,0:T(8,128)(2,1)}, f32[1,2048]{1,0:T(1,128)S(1)}) custom-call(bf16[4,2,2,2,64,2048]{5,4,3,2,1,0:T(8,128)(2,1)} %bitcast.85, f32[1]{0:T(128)} %bitcast.75.lam_ref), custom_call_target="tpu_custom_call" | custom-call | tf_op jit(solution)/shard_map/pallas_call | solution.py:267
  201.6 0.0 slice-start.1
  201.6 7.1 %convolution_bitcast_fusion = f32[1,512,2048]{2,1,0:T(8,128)S(1)} fusion(bf16[2048,2048]{1,0:T(8,128)(2,1)} %bitcast.87, bf16[2,512,2048]{2,1,0:T(8,128)(2,1)S(1)} %fusion.10), kind=kOutput, calls=%fused_computation.36 | convolution fusion | flops 4294967296 | bytes 14680064 | tf_op jit(solution)/shard_map/dot_general | solution.py:321
  208.7 9.1 %convolution_bitcast_fusion.1 = f32[1,512,2048]{2,1,0:T(8,128)S(1)} fusion(bf16[2048,2048]{1,0:T(8,128)(2,1)} %bitcast.88, bf16[2,512,2048]{2,1,0:T(8,128)(2,1)} %copy-done.3), kind=kOutput, calls=%fused_computation.37 | convolution fusion | flops 4294967296 | bytes 14680064 | tf_op jit(solution)/shard_map/dot_general | solution.py:319
  217.9 2.2 fusion.11
  220.1 0.7 pad_maximum_fusion.1.in_ref
  220.8 18.0 %shard_map.165 = f32[5,2048]{1,0:T(8,128)} custom-call(f32[5,2048]{1,0:T(8,128)} %pad_maximum_fusion.1.in_ref), custom_call_target="tpu_custom_call" | custom-call | tf_op jit(solution)/shard_map/pallas_call | solution.py:83
  238.8 1.5 slice_reduce_fusion
  240.2 0.9 fusion.20
  241.2 7.4 %multiply_convert_fusion.2 = bf16[2,512,2048]{2,1,0:T(8,128)(2,1)S(1)} fusion(f32[2,512,2048]{2,1,0:T(8,128)} %get-tuple-element.42, f32[1,512,2048]{2,1,0:T(8,128)} %copy-done, f32[1,512,2048]{2,1,0:T(8,128)} %copy-done.1, f32[2,2048]{1,0:T(2,128)S(1)} %get-tuple-element.29, f32[2,2048]{1,0:T(2,128)S(1)} %get-tuple-element.28, ...), kind=kLoop, calls=%fused_computation.20 | loop fusion | flops 18874368 | bytes 21037056 | tf_op jit(solution)/shard_map/convert_element_type | solution.py:325
  248.6 13.3 %bitcast_convert_fusion = bf16[2048,2048]{1,0:T(8,128)(2,1)S(1)} fusion(bf16[2,512,2048]{2,1,0:T(8,128)(2,1)S(1)} %multiply_convert_fusion.2, f32[2,512,2048]{2,1,0:T(8,128)} %get-tuple-element.41, f32[2048]{0:T(1024)S(1)} %copy-done.9, f32[2,2048]{1,0:T(2,128)S(1)} %get-tuple-element.37, f32[2,2048]{1,0:T(2,128)S(1)} %get-tuple-element.36, f32[2048]{0:T(1024)S(1)} %copy-done.6), kind=kOutput, calls=%fused_computation | convolution fusion | flops 8606711808 | bytes 21020672 | tf_op jit(solution)/shard_map/dot_general | solution.py:327
  261.9 52.2 %shard_map.170 = f32[64,2048]{1,0:T(8,128)S(1)} custom-call(bf16[4,2,2,2,64,2048]{5,4,3,2,1,0:T(8,128)(2,1)S(1)} %bitcast.77), custom_call_target="tpu_custom_call" | custom-call | tf_op jit(solution)/shard_map/pallas_call | solution.py:195
  314.2 16.2 %fusion.17 = (f32[2,2048]{1,0:T(2,128)S(1)}, f32[2,2048]{1,0:T(2,128)S(1)}, f32[2,512,2048]{2,1,0:T(8,128)}) fusion(f32[2,2048]{1,0:T(2,128)S(1)} %get-tuple-element.37, f32[2,512,2048]{2,1,0:T(8,128)S(1)} %bitcast.84, f32[2,2048]{1,0:T(2,128)S(1)} %get-tuple-element.36, bf16[2,512,2048]{2,1,0:T(8,128)(2,1)} %copy-done.2, bf16[2048,2048]{1,0:T(8,128)(2,1)} %param.14, ...), kind=kOutput, calls=%fused_computation.60 | convolution fusion | flops 8608800768 | bytes 29442048 | tf_op jit(solution)/shard_map/dot_general | solution.py:328
  330.4 0.6 pad_maximum_fusion.5.in_ref
  331.0 14.2 %shard_map.166 = f32[4,2048]{1,0:T(4,128)} custom-call(f32[4,2048]{1,0:T(4,128)} %pad_maximum_fusion.5.in_ref), custom_call_target="tpu_custom_call" | custom-call | tf_op jit(solution)/shard_map/pallas_call | solution.py:83
  345.2 1.5 slice_reduce_fusion.4
  346.7 8.8 %multiply_convert_fusion.1 = bf16[2,512,2048]{2,1,0:T(8,128)(2,1)} fusion(f32[2,512,2048]{2,1,0:T(8,128)} %get-tuple-element.43, f32[2,512,2048]{2,1,0:T(8,128)} %get-tuple-element.41, f32[2,2048]{1,0:T(2,128)S(1)} %get-tuple-element.30, f32[2,2048]{1,0:T(2,128)S(1)} %get-tuple-element.31, f32[2,2048]{1,0:T(2,128)S(1)} %get-tuple-element.37, ...), kind=kLoop, calls=%fused_computation.18 | loop fusion | flops 18874368 | bytes 21045248 | tf_op jit(solution)/shard_map/convert_element_type | solution.py:331
  355.5 13.1 %bitcast_convert_fusion.1 = bf16[2048,2048]{1,0:T(8,128)(2,1)S(1)} fusion(bf16[2,512,2048]{2,1,0:T(8,128)(2,1)} %multiply_convert_fusion.1, f32[1024,2048]{1,0:T(8,128)} %get-tuple-element.40, f32[2048]{0:T(1024)S(1)} %copy-done.10, f32[2,2048]{1,0:T(2,128)S(1)} %get-tuple-element.39, f32[2,2048]{1,0:T(2,128)S(1)} %get-tuple-element.38, f32[2048]{0:T(1024)S(1)} %copy-done.7), kind=kOutput, calls=%fused_computation.1 | convolution fusion | flops 8606711808 | bytes 21020672 | tf_op jit(solution)/shard_map/dot_general | solution.py:333
  368.6 51.0 %shard_map.169 = f32[64,2048]{1,0:T(8,128)S(1)} custom-call(bf16[4,2,2,2,64,2048]{5,4,3,2,1,0:T(8,128)(2,1)S(1)} %bitcast.78), custom_call_target="tpu_custom_call" | custom-call | tf_op jit(solution)/shard_map/pallas_call | solution.py:195
  419.6 15.8 %fusion.16 = (f32[2,2048]{1,0:T(2,128)S(1)}, f32[2,2048]{1,0:T(2,128)S(1)}, f32[2,512,2048]{2,1,0:T(8,128)}) fusion(f32[2,2048]{1,0:T(2,128)S(1)} %get-tuple-element.39, f32[2,2048]{1,0:T(2,128)S(1)} %get-tuple-element.38, f32[1024,2048]{1,0:T(8,128)S(1)} %bitcast.82, bf16[2,512,2048]{2,1,0:T(8,128)(2,1)} %multiply_convert_fusion.1, ...), kind=kOutput, calls=%fused_computation.59 | convolution fusion | flops 8608800768 | bytes 29442048 | tf_op jit(solution)/shard_map/dot_general | solution.py:334
  435.4 0.6 pad_maximum_fusion.6.in_ref
  436.0 12.7 %shard_map.167 = f32[4,2048]{1,0:T(4,128)} custom-call(f32[4,2048]{1,0:T(4,128)} %pad_maximum_fusion.6.in_ref), custom_call_target="tpu_custom_call" | custom-call | tf_op jit(solution)/shard_map/pallas_call | solution.py:83
  448.7 1.5 slice_reduce_fusion.2
  450.2 7.2 %multiply_convert_fusion = bf16[2,512,2048]{2,1,0:T(8,128)(2,1)S(1)} fusion(f32[2,512,2048]{2,1,0:T(8,128)} %get-tuple-element.44, f32[1024,2048]{1,0:T(8,128)} %get-tuple-element.40, f32[2,2048]{1,0:T(2,128)S(1)} %get-tuple-element.32, f32[2,2048]{1,0:T(2,128)S(1)} %get-tuple-element.33, f32[2,2048]{1,0:T(2,128)S(1)} %get-tuple-element.39, ...), kind=kLoop, calls=%fused_computation.16 | loop fusion | flops 18874368 | bytes 21045248 | tf_op jit(solution)/shard_map/convert_element_type | solution.py:337
  457.5 9.7 %convolution_convert_fusion = bf16[2048,2048]{1,0:T(8,128)(2,1)S(1)} fusion(bf16[1024,2048]{1,0:T(8,128)(2,1)S(1)} %copy-done.5, bf16[1024,2048]{1,0:T(8,128)(2,1)S(1)} %bitcast.86), kind=kOutput, calls=%fused_computation.32 | convolution fusion | flops 8594128896 | bytes 16777216 | tf_op jit(solution)/shard_map/dot_general | solution.py:339
  467.2 51.5 %shard_map.168 = f32[64,2048]{1,0:T(8,128)S(1)} custom-call(bf16[4,2,2,2,64,2048]{5,4,3,2,1,0:T(8,128)(2,1)S(1)} %bitcast.76), custom_call_target="tpu_custom_call" | custom-call | tf_op jit(solution)/shard_map/pallas_call | solution.py:195
  518.7 0.8 copy.27
  519.5 0.8 copy.28
  520.3 0.8 copy.29
  (33 shorter events, 0.1 us)
Async XLA Ops:
  1.3 4.6 copy-start.8
  5.9 11.1 %copy-start.4 = (bf16[1024,2048]{1,0:T(8,128)(2,1)}, bf16[1024,2048]{1,0:T(8,128)(2,1)S(1)}, u32[]{:S(2)}) copy-start(bf16[1024,2048]{1,0:T(8,128)(2,1)S(1)} %constant_dynamic-update-slice_fusion) | copy-start | bytes 12582916
  5.9 27.7 %copy-start.7 = (f32[2048]{0:T(1024)S(1)}, f32[2048]{0:T(1024)}, u32[]{:S(2)}) copy-start(f32[2048]{0:T(1024)} %param.15) | copy-start | bytes 24580
  5.9 27.7 %copy-start.10 = (f32[2048]{0:T(1024)S(1)}, f32[2048]{0:T(1024)}, u32[]{:S(2)}) copy-start(f32[2048]{0:T(1024)} %param.16) | copy-start | bytes 24580
  33.6 30.1 %copy-start.6 = (f32[2048]{0:T(1024)S(1)}, f32[2048]{0:T(1024)}, u32[]{:S(2)}) copy-start(f32[2048]{0:T(1024)} %param.17) | copy-start | bytes 24580
  33.6 30.1 %copy-start.9 = (f32[2048]{0:T(1024)S(1)}, f32[2048]{0:T(1024)}, u32[]{:S(2)}) copy-start(f32[2048]{0:T(1024)} %param.18) | copy-start | bytes 24580
  97.7 103.8 %copy-start.3 = (bf16[2,512,2048]{2,1,0:T(8,128)(2,1)}, bf16[2,512,2048]{2,1,0:T(8,128)(2,1)S(1)}, u32[]{:S(2)}) copy-start(bf16[2,512,2048]{2,1,0:T(8,128)(2,1)S(1)} %fusion.10) | copy-start | bytes 12582916
  104.6 113.2 %slice-start = ((s8[8388608]{0:T(1024)(128)(4,1)}), s8[4194304]{0:T(1024)(128)(4,1)S(1)}, s32[]{:S(2)}) async-start(s8[8388608]{0:T(1024)(128)(4,1)} %bitcast.79), calls=%async_computation | async-start | bytes 8388608
  201.6 16.3 %slice-start.1 = ((s8[8388608]{0:T(1024)(128)(4,1)}), s8[4194304]{0:T(1024)(128)(4,1)S(1)}, s32[]{:S(2)}) async-start(s8[8388608]{0:T(1024)(128)(4,1)} %bitcast.79), calls=%async_computation.1 | async-start | bytes 8388608
  208.7 9.2 %copy-start = (f32[1,512,2048]{2,1,0:T(8,128)}, f32[1,512,2048]{2,1,0:T(8,128)S(1)}, u32[]{:S(2)}) copy-start(f32[1,512,2048]{2,1,0:T(8,128)S(1)} %convolution_bitcast_fusion) | copy-start | bytes 12582916
  217.9 2.2 copy-start.1
  241.2 73.0 %slice-start.4 = ((s8[8388608]{0:T(1024)(128)(4,1)}), s8[4194304]{0:T(1024)(128)(4,1)S(1)}, s32[]{:S(2)}) async-start(s8[8388608]{0:T(1024)(128)(4,1)} %bitcast.83), calls=%async_computation.4 | async-start | bytes 8388608
  248.6 13.3 %copy-start.2 = (bf16[2,512,2048]{2,1,0:T(8,128)(2,1)}, bf16[2,512,2048]{2,1,0:T(8,128)(2,1)S(1)}, u32[]{:S(2)}) copy-start(bf16[2,512,2048]{2,1,0:T(8,128)(2,1)S(1)} %multiply_convert_fusion.2) | copy-start | bytes 12582916
  248.6 65.5 %slice-start.5 = ((s8[8388608]{0:T(1024)(128)(4,1)}), s8[4194304]{0:T(1024)(128)(4,1)S(1)}, s32[]{:S(2)}) async-start(s8[8388608]{0:T(1024)(128)(4,1)} %bitcast.83), calls=%async_computation.5 | async-start | bytes 8388608
  346.7 72.9 %slice-start.2 = ((s8[8388608]{0:T(1024)(128)(4,1)}), s8[4194304]{0:T(1024)(128)(4,1)S(1)}, s32[]{:S(2)}) async-start(s8[8388608]{0:T(1024)(128)(4,1)} %bitcast.81), calls=%async_computation.2 | async-start | bytes 8388608
  355.5 64.1 %slice-start.3 = ((s8[8388608]{0:T(1024)(128)(4,1)}), s8[4194304]{0:T(1024)(128)(4,1)S(1)}, s32[]{:S(2)}) async-start(s8[8388608]{0:T(1024)(128)(4,1)} %bitcast.81), calls=%async_computation.3 | async-start | bytes 8388608
  450.2 7.3 %copy-start.5 = (bf16[1024,2048]{1,0:T(8,128)(2,1)S(1)}, bf16[1024,2048]{1,0:T(8,128)(2,1)}, u32[]{:S(2)}) copy-start(bf16[1024,2048]{1,0:T(8,128)(2,1)} %copy-done.4) | copy-start | bytes 12582916

commit v2 on v1

--- a/solution.py
+++ b/solution.py
@@ -8,9 +8,7 @@
 from jax.sharding import PartitionSpec as P
 
 NORM_EPS = 1e-5
-ROW_DIMS = (((0, 1), (0, 1)), ((), ()))
 FIRST_DIMS = (((0,), (0,)), ((), ()))
-LAST_DIMS = (((2,), (1,)), ((), ()))
 MESH = pl.DeviceIdType.MESH
 F32 = jnp.float32
 BF16 = jnp.bfloat16
@@ -172,37 +170,6 @@
     ]
 
 
-def scatter_kernel(chunks, part_ref, out_ref, *scratch):
-    at = Place()
-    enter([at.partner, at.x_peer, at.y_peer] + at.z_peers)
-    send_sem, recv_sem = scratch[7:]
-    chunk = part_ref.shape[-1] // chunks
-    scatter = Scatter(at, part_ref, scratch[:7], send_sem, recv_sem, chunk)
-    for j in range(chunks):
-        scatter.stage0(j)
-    for t in range(chunks + 3):
-        for stage, step in enumerate((scatter.stage1, scatter.stage2, scatter.stage3)):
-            if 0 <= t - stage < chunks:
-                step(t - stage)
-        j = t - 3
-        if j >= 0:
-            out_ref[:, scatter.cols(j)] = scatter.final(j)
-
-
-def scatter_sum(part, collective_id, chunks=8):
-    full, cols = part.shape
-    rows = full // 32
-    return pl.pallas_call(
-        functools.partial(scatter_kernel, chunks),
-        out_shape=jax.ShapeDtypeStruct((rows, cols), F32),
-        in_specs=[pl.BlockSpec(memory_space=pltpu.VMEM)],
-        out_specs=pl.BlockSpec(memory_space=pltpu.VMEM),
-        scratch_shapes=scatter_scratch(rows, cols, chunks, 6),
-        compiler_params=pltpu.CompilerParams(
-            collective_id=collective_id, has_side_effects=True, vmem_limit_bytes=40 * 2**20),
-    )(part.reshape(4, 2, 2, 2, rows, cols))
-
-
 def corr_kernel(chunks, total_rows, part_ref, lam_ref, grad_ref, loss_ref, *scratch):
     at = Place()
     enter([at.partner, at.x_peer, at.y_peer] + at.z_peers)
@@ -276,6 +243,372 @@
     return grad.reshape(full, cols), loss
 
 
+class Sums:
+    def __init__(self, at, local, total, recv0, slots1, slots2, send_sem, recv_sem):
+        self.at, self.local, self.total = at, local, total
+        self.recv0, self.slots1, self.slots2 = recv0, slots1, slots2
+        self.send_sem, self.recv_sem = send_sem, recv_sem
+        half = local.shape[-1] // 2
+        self.mine = pl.ds(pl.multiple_of(at.core * half, 128), half)
+        self.theirs = pl.ds(pl.multiple_of((1 - at.core) * half, 128), half)
+        self.copies = []
+
+    def start(self, k, src, dst, peer):
+        copy = remote(src, dst, self.send_sem.at[k], self.recv_sem.at[k], peer)
+        copy.start()
+        self.copies.append(copy)
+
+    def arrive(self):
+        for copy in self.copies:
+            copy.wait()
+        self.copies = []
+
+    def begin(self):
+        self.start(0, self.local.at[:, self.theirs], self.recv0, self.at.partner)
+
+    def over_plane(self):
+        self.arrive()
+        here = self.slots1.at[self.at.plane]
+        here[...] = self.local[:, self.mine] + self.recv0[...]
+        for d in range(3):
+            self.start(1 + d, here, here, self.at.plane_peers[d])
+
+    def over_line(self):
+        self.arrive()
+        here = self.slots2.at[self.at.z]
+        here[...] = (self.slots1[0] + self.slots1[1]) + (self.slots1[2] + self.slots1[3])
+        for d in range(3):
+            self.start(4 + d, here, here, self.at.z_peers[d])
+
+    def over_pair(self):
+        self.arrive()
+        here = self.total.at[:, self.mine]
+        here[...] = (self.slots2[0] + self.slots2[1]) + (self.slots2[2] + self.slots2[3])
+        self.start(7, here, here, self.at.partner)
+
+
+def sums_scratch(rows, cols):
+    return [
+        pltpu.VMEM((rows, cols // 2), F32),
+        pltpu.VMEM((4, rows, cols // 2), F32),
+        pltpu.VMEM((4, rows, cols // 2), F32),
+        pltpu.SemaphoreType.DMA((8,)),
+        pltpu.SemaphoreType.DMA((8,)),
+    ]
+
+
+class Ring:
+    def __init__(self, at, chunks, total, part, recv0, kept, snd1, recv1, snd2, recv2, snd3, recv3, send_sem, recv_sem, credit):
+        self.at, self.chunks, self.total_chunks = at, chunks, total
+        self.part, self.recv0, self.kept = part, recv0, kept
+        self.snd1, self.recv1, self.snd2, self.recv2, self.snd3, self.recv3 = snd1, recv1, snd2, recv2, snd3, recv3
+        self.send_sem, self.recv_sem, self.credit = send_sem, recv_sem, credit
+        self.copies = {}
+
+    def start(self, q, stage, src, dst, peer, again):
+        j = q % self.chunks
+        if q >= again:
+            pl.semaphore_wait(self.credit.at[j if again > 2 else q % 2, stage], 1)
+        copy = remote(src, dst, self.send_sem.at[j, stage], self.recv_sem.at[j, stage], peer)
+        copy.start()
+        self.copies[q, stage] = copy
+
+    def give(self, q, stage, peer, again):
+        if q + again < self.total_chunks:
+            slot = q % self.chunks if again > 2 else q % 2
+            pl.semaphore_signal(self.credit.at[slot, stage], inc=1, device_id=(peer,), device_id_type=MESH)
+
+    def pair(self, q):
+        at, s = self.at, q % 2
+        self.start(q, 0, self.part.at[s, :, :, :, 1 - at.core], self.recv0.at[s], at.partner, 2)
+
+    def first(self, q):
+        at, s, j = self.at, q % 2, q % self.chunks
+        self.copies[q, 0].wait()
+
+        @pl.loop(0, 4)
+        def _(z):
+            for k in range(2):
+                (y, x), (oy, ox) = ((k, at.x), (k, 1 - at.x)) if q % 2 == 0 else ((at.y, k), (1 - at.y, k))
+                self.snd1[j, z, k] = (self.part[s, z, oy, ox, at.core] + self.recv0[s, z, oy, ox]).astype(BF16)
+                self.kept[j, z, k] = self.part[s, z, y, x, at.core] + self.recv0[s, z, y, x]
+
+        self.give(q, 0, at.partner, 2)
+        self.start(q, 1, self.snd1.at[j], self.recv1.at[j], at.x_peer if q % 2 == 0 else at.y_peer, self.chunks)
+
+    def second(self, q):
+        at, j = self.at, q % self.chunks
+        own = at.y if q % 2 == 0 else at.x
+        self.copies[q, 1].wait()
+
+        @pl.loop(0, 4)
+        def _(z):
+            self.snd2[j, z] = (self.kept[j, z, 1 - own] + self.recv1[j, z, 1 - own].astype(F32)).astype(BF16)
+            self.kept[j, z, own] = self.kept[j, z, own] + self.recv1[j, z, own].astype(F32)
+
+        self.give(q, 1, at.x_peer if q % 2 == 0 else at.y_peer, self.chunks)
+        self.start(q, 2, self.snd2.at[j], self.recv2.at[j], at.y_peer if q % 2 == 0 else at.x_peer, self.chunks)
+
+    def third(self, q):
+        at, j = self.at, q % self.chunks
+        own = at.y if q % 2 == 0 else at.x
+        self.copies[q, 2].wait()
+        for d in range(3):
+            z = lax.rem(at.z + d + 1, 4)
+            self.snd3[j, d] = (self.kept[j, z, own] + self.recv2[j, z].astype(F32)).astype(BF16)
+            self.start(q, 3 + d, self.snd3.at[j, d], self.recv3.at[j, d], at.z_peers[d], self.chunks)
+
+    def last(self, q):
+        at, j = self.at, q % self.chunks
+        own = at.y if q % 2 == 0 else at.x
+        total = self.kept[j, at.z, own] + self.recv2[j, at.z].astype(F32)
+        self.give(q, 2, at.y_peer if q % 2 == 0 else at.x_peer, self.chunks)
+        for d in range(3):
+            self.copies[q, 3 + d].wait()
+            total += self.recv3[j, d].astype(F32)
+            self.give(q, 3 + d, at.z_peers[2 - d], self.chunks)
+        return total
+
+
+def ring_scratch(chunks, rows, width):
+    return [
+        pltpu.VMEM((2, 4, 2, 2, 2, rows, width), F32),
+        pltpu.VMEM((2, 4, 2, 2, rows, width), F32),
+        pltpu.VMEM((chunks, 4, 2, rows, width), F32),
+        pltpu.VMEM((chunks, 4, 2, rows, width), BF16),
+        pltpu.VMEM((chunks, 4, 2, rows, width), BF16),
+        pltpu.VMEM((chunks, 4, rows, width), BF16),
+        pltpu.VMEM((chunks, 4, rows, width), BF16),
+        pltpu.VMEM((chunks, 3, rows, width), BF16),
+        pltpu.VMEM((chunks, 3, rows, width), BF16),
+        pltpu.SemaphoreType.DMA((chunks, 6)),
+        pltpu.SemaphoreType.DMA((chunks, 6)),
+        pltpu.SemaphoreType.REGULAR((chunks, 6)),
+    ]
+
+
+CHUNKS = 8
+RING = 12
+SUMS = 5
+
+
+def backward_kernel(
+        total_rows, embed_sums, grad_embed, embed, norm_two, norm_one, act_two, act_one,
+        act_two_t, act_one_t, feat_t, w_three, w_two, scale_three, scale_two, scale_one,
+        grad_w_three, grad_w_two, grad_w_one, total_three, total_two, total_one,
+        grad, pre, turned, weight, normed, act, local, w_sem, load_sem, *scratch):
+    at = Place()
+    enter([at.partner] + at.plane_peers + at.z_peers)
+    ring = Ring(at, CHUNKS, 3 * CHUNKS, *scratch[:RING])
+    dim = grad.shape[1]
+    width = dim // CHUNKS
+    view_rows = grad.shape[0] // 2
+    block_rows = min(64, view_rows)
+    count = 1.0 / total_rows
+    feeds = [act_two_t, act_one_t, feat_t]
+    norms = [embed, norm_two, norm_one]
+    masks = [act_two, act_one]
+    weights = [w_three, w_two]
+    scales = [scale_three, scale_two, scale_one]
+    outs = [grad_w_three, grad_w_two, grad_w_one]
+    totals = [total_three, total_two, total_one]
+    sums = {}
+    sums[0, 0] = Sums(at, embed_sums, total_three, *scratch[RING:RING + SUMS])
+    for layer in (1, 2):
+        for h in range(2):
+            first = RING + SUMS * (2 * layer - 1 + h)
+            sums[layer, h] = Sums(at, local.at[layer - 1, h], totals[layer].at[h], *scratch[first:first + SUMS])
+
+    def load(src, dst, k):
+        copy = pltpu.make_async_copy(src, dst, load_sem.at[k])
+        copy.start()
+        return copy
+
+    sums[0, 0].begin()
+    loads = {
+        "pre": load(grad_embed, pre, 0),
+        ("norm", 0): load(embed, normed.at[0], 1),
+        ("feed", 0): load(act_two_t, turned.at[0], 3),
+        ("norm", 1): load(norm_two, normed.at[1], 2),
+        ("act", 0): load(act_two, act, 5),
+    }
+    slots = weight.shape[0]
+    w_loads = {}
+
+    def load_weight(layer, n):
+        copy = pltpu.make_async_copy(weights[layer].at[pl.ds(n * width, width), :], weight.at[n % slots],
+                                     w_sem.at[n % slots])
+        copy.start()
+        w_loads[layer, n] = copy
+
+    for n in range(slots):
+        load_weight(0, n)
+    sums[0, 0].over_plane()
+    sums[0, 0].over_line()
+    sums[0, 0].over_pair()
+
+    def finish_grad(layer, j):
+        cols = pl.ds(j * width, width)
+        total, first = (total_three, j * width) if layer == 0 else (
+            totals[layer].at[j // (CHUNKS // 2)], (j % (CHUNKS // 2)) * width)
+        sel = pl.ds(first, width)
+        for v in range(2):
+            mean0 = total[v:v + 1, sel] * count
+            mean1 = total[2 + v:3 + v, sel] * count
+            scale = scales[layer][v:v + 1, cols]
+
+            @pl.loop(0, view_rows // block_rows)
+            def _(r):
+                rows = pl.ds(pl.multiple_of(v * view_rows + r * block_rows, block_rows), block_rows)
+                xhat = normed[layer % 2, rows, cols].astype(F32)
+                grad[rows, cols] = (scale * (pre[rows, cols] - (mean0 + xhat * mean1))).astype(BF16)
+
+    def weight_grad(layer, j):
+        cols = pl.ds(j * width, width)
+        s = j % 2
+
+        @pl.loop(0, 4)
+        def _(z):
+            rows = pl.ds(pl.multiple_of(z * (dim // 4), dim // 4), dim // 4)
+            out = jnp.dot(turned[layer % 2, rows, :], grad[:, cols], preferred_element_type=F32)
+            ring.part[s, z] = out.reshape(ring.part.shape[2:])
+
+        ring.pair(layer * CHUNKS + j)
+
+    def input_grad(layer, n):
+        cols = pl.ds(n * width, width)
+        w_loads[layer, n].wait()
+        half = local.at[layer, n // (CHUNKS // 2)]
+        sel = pl.ds((n % (CHUNKS // 2)) * width, width)
+
+        @pl.loop(0, 2)
+        def _(v):
+            rows = pl.ds(pl.multiple_of(v * view_rows, view_rows), view_rows)
+            out = lax.dot_general(grad[rows, :], weight[n % slots], (((1,), (1,)), ((), ())),
+                                  preferred_element_type=F32)
+            out = jnp.where(act[rows, cols] > 0, out, 0.0)
+            pre[rows, cols] = out
+            half[pl.ds(v, 1), sel] = jnp.sum(out, axis=0, keepdims=True)
+            half[pl.ds(2 + v, 1), sel] = jnp.sum(out * normed[(layer + 1) % 2, rows, cols].astype(F32), axis=0, keepdims=True)
+
+        if n + slots < CHUNKS:
+            load_weight(layer, n + slots)
+
+    last = 3 * CHUNKS - 1
+
+    def serve(q):
+        if q <= last:
+            ring.first(q)
+        if 0 <= q - 2 <= last:
+            ring.second(q - 2)
+        if 0 <= q - 3 <= last:
+            ring.third(q - 3)
+        if 0 <= q - 5 <= last:
+            done = q - 5
+            outs[done // CHUNKS][:, pl.ds((done % CHUNKS) * width, width)] = ring.last(done)
+
+    for layer in range(3):
+        q = layer * CHUNKS
+        if layer == 0:
+            sums[0, 0].arrive()
+            loads["pre"].wait()
+        else:
+            sums[layer, 0].arrive()
+        if layer == 0:
+            loads["norm", 0].wait()
+        finish_grad(layer, 0)
+        loads["feed", layer].wait()
+        weight_grad(layer, 0)
+        if layer < 2:
+            loads["feed", layer + 1] = load(feeds[layer + 1], turned.at[(layer + 1) % 2], 3 + (layer + 1) % 2)
+        if layer > 0:
+            sums[layer, 1].over_pair()
+        serve(q)
+        finish_grad(layer, 1)
+        weight_grad(layer, 1)
+        serve(q + 1)
+        finish_grad(layer, 2)
+        weight_grad(layer, 2)
+        finish_grad(layer, 3)
+        if layer > 0:
+            sums[layer, 1].arrive()
+        for j in range(4, CHUNKS):
+            finish_grad(layer, j)
+        if layer == 0:
+            loads["norm", 2] = load(norm_one, normed.at[0], 1)
+        serve(q + 2)
+        if layer == 2:
+            for j in range(3, CHUNKS):
+                weight_grad(layer, j)
+                serve(q + j)
+            break
+        loads["norm", layer + 1].wait()
+        loads["act", layer].wait()
+        input_grad(layer, 0)
+        input_grad(layer, 1)
+        weight_grad(layer, 3)
+        input_grad(layer, 2)
+        serve(q + 3)
+        input_grad(layer, 3)
+        sums[layer + 1, 0].begin()
+        weight_grad(layer, 4)
+        sums[layer + 1, 0].over_plane()
+        input_grad(layer, 4)
+        serve(q + 4)
+        input_grad(layer, 5)
+        sums[layer + 1, 0].over_line()
+        weight_grad(layer, 5)
+        input_grad(layer, 6)
+        serve(q + 5)
+        input_grad(layer, 7)
+        sums[layer + 1, 1].begin()
+        if layer == 0:
+            loads["act", 1] = load(masks[1], act, 5)
+            for n in range(slots):
+                load_weight(1, n)
+        sums[layer + 1, 0].over_pair()
+        weight_grad(layer, 6)
+        sums[layer + 1, 1].over_plane()
+        serve(q + 6)
+        weight_grad(layer, 7)
+        sums[layer + 1, 1].over_line()
+        serve(q + 7)
+    for q in range(3 * CHUNKS, 3 * CHUNKS + 5):
+        serve(q)
+
+
+def backward(total_rows, vmem, *args):
+    grad_embed = args[1]
+    rows, dim = grad_embed.shape
+    width, blocks = dim // CHUNKS, dim // 32
+    hbm = pl.BlockSpec(memory_space=pl.ANY)
+    vm = pl.BlockSpec(memory_space=pltpu.VMEM)
+    scratch = [
+        pltpu.VMEM((rows, dim), BF16),
+        pltpu.VMEM((rows, dim), F32),
+        pltpu.VMEM((2, dim, rows), BF16),
+        pltpu.VMEM((3, width, dim), BF16),
+        pltpu.VMEM((2, rows, dim), BF16),
+        pltpu.VMEM((rows, dim), BF16),
+        pltpu.VMEM((2, 2, 4, dim // 2), F32),
+        pltpu.SemaphoreType.DMA((3,)),
+        pltpu.SemaphoreType.DMA((6,)),
+    ] + ring_scratch(CHUNKS, blocks, width) + sums_scratch(5, dim)
+    for _ in range(4):
+        scratch += sums_scratch(4, dim // 2)
+    return pl.pallas_call(
+        functools.partial(backward_kernel, total_rows),
+        out_shape=[jax.ShapeDtypeStruct((blocks, dim), F32)] * 3 + [
+            jax.ShapeDtypeStruct((5, dim), F32),
+            jax.ShapeDtypeStruct((2, 4, dim // 2), F32),
+            jax.ShapeDtypeStruct((2, 4, dim // 2), F32)],
+        in_specs=[vm] + [hbm] * 11 + [vm] * 3,
+        out_specs=[vm] * 6,
+        scratch_shapes=scratch,
+        compiler_params=pltpu.CompilerParams(collective_id=5, has_side_effects=True, vmem_limit_bytes=vmem),
+    )(*args)
+
+
 def norm_forward(values, total_rows, collective_id):
     cols = values.shape[-1]
     col_sums = jnp.concatenate([jnp.sum(values, axis=1), jnp.sum(values * values, axis=1)])
@@ -283,17 +616,6 @@
     col_mean = col_sums[0] / total_rows
     inv_std = lax.rsqrt(col_sums[1] / total_rows - col_mean * col_mean + NORM_EPS)
     return (values - col_mean[:, None, :]) * inv_std[:, None, :], inv_std
-
-
-def norm_backward(grad_out, normed, inv_std, total_rows, collective_id, extra=None):
-    cols = grad_out.shape[-1]
-    rows = [jnp.sum(grad_out, axis=1), jnp.sum(grad_out * normed, axis=1)]
-    if extra is not None:
-        rows.append(extra)
-    summed = all_sums(jnp.concatenate(rows), collective_id)
-    col_sums = summed[:4].reshape(2, 2, cols)
-    grad_in = inv_std[:, None, :] * (grad_out - (col_sums[0][:, None, :] + normed * col_sums[1][:, None, :]) / total_rows)
-    return grad_in, col_sums, summed[4:]
 
 
 def solution(mesh):
@@ -319,27 +641,20 @@
         grad_embed_a = lax.dot_general(embed_pair[1], grad_scaled, (((1,), (1,)), ((), ())),
                                        preferred_element_type=F32)
         grad_embed_b = jnp.dot(embed_pair[0], grad_scaled, preferred_element_type=F32)
-        grad_embed = jnp.stack([grad_embed_a, grad_embed_b])
-        grad_proj, _, loss_cols = norm_backward(grad_embed, normed_out, inv_out, total_rows, 4, loss_cols)
-        loss_total = jnp.sum(loss_cols)
-        grad_proj = grad_proj.astype(BF16)
-        grad_w_three = scatter_sum(
-            lax.dot_general(act_two, grad_proj, ROW_DIMS, preferred_element_type=F32).astype(BF16), 5)
-        grad_act_two = lax.dot_general(grad_proj, w_three, LAST_DIMS, preferred_element_type=F32)
-        grad_pre_two = jnp.where(pre_two > 0, grad_act_two, 0.0)
-        grad_hidden_two, sums_two, _ = norm_backward(grad_pre_two, normed_two, inv_two, total_rows, 6)
-        grad_hidden_two = (gain_two * grad_hidden_two).astype(BF16)
-        grad_w_two = scatter_sum(
-            lax.dot_general(act_one, grad_hidden_two, ROW_DIMS, preferred_element_type=F32).astype(BF16), 7)
-        grad_act_one = lax.dot_general(grad_hidden_two, w_two, LAST_DIMS, preferred_element_type=F32)
-        grad_pre_one = jnp.where(pre_one > 0, grad_act_one, 0.0)
-        grad_hidden_one, sums_one, _ = norm_backward(grad_pre_one, normed_one, inv_one, total_rows, 8)
-        grad_hidden_one = (gain_one * grad_hidden_one).astype(BF16).reshape(2 * rows_dev, -1)
-        grad_w_one = scatter_sum(
-            lax.dot_general(feat_rows, grad_hidden_one, FIRST_DIMS, preferred_element_type=F32).astype(BF16), 9)
+        grad_embed = jnp.concatenate([grad_embed_a, grad_embed_b])
+        products = grad_embed.reshape(2, rows_dev, -1)
+        embed_sums = jnp.concatenate(
+            [jnp.sum(products, axis=1), jnp.sum(products * embed_pair.astype(F32), axis=1), loss_cols])
+        flat = lambda values: values.reshape(2 * rows_dev, -1)
+        act_one, act_two = flat(act_one), flat(act_two)
+        grad_w_three, grad_w_two, grad_w_one, total_three, total_two, total_one = backward(
+            total_rows, 62 * 2**20, embed_sums, grad_embed, flat(embed_pair), flat(normed_two.astype(BF16)),
+            flat(normed_one.astype(BF16)), act_two, act_one, act_two.T, act_one.T, feat_rows.T, w_three, w_two,
+            inv_out, gain_two * inv_two, gain_one * inv_one)
+        loss_total = jnp.sum(total_three[4])
+        both = lambda total, row: (total[:, row] + total[:, row + 1]).reshape(-1)
         return (loss_total, grad_w_one, grad_w_two, grad_w_three,
-                jnp.sum(sums_one[1], axis=0), jnp.sum(sums_one[0], axis=0),
-                jnp.sum(sums_two[1], axis=0), jnp.sum(sums_two[0], axis=0))
+                both(total_one, 2), both(total_one, 0), both(total_two, 2), both(total_two, 0))
 
     row_spec = P("data", None)
     whole_mat = P(None, None)

time: 531 us -> 502 us (0.945)
  matrix products: 134 us -> 69.3 us
  local copies, waits for them, and re-layouts: 8 us -> 68.2 us
  Pallas kernels: 336 us -> 307 us
  other arithmetic: 41.1 us -> 47.9 us
    dot_general x5 -> x0, matrix products: 68 us -> none  [the longest x1 16.2 us: local_step(): lax.dot_general(grad_proj, w_three, LAST_DIMS, preferred_element_type=F32)]
    pallas_call x6 -> x3, Pallas kernels: 84.7 us -> 39.8 us  [all_sums(): pl.pallas_call(sums_kernel, out_shape=jax.ShapeDtypeStruct(values.shape,...]
    pallas_call x3 -> x1, Pallas kernels: 155 us -> 169 us  [backward(): pl.pallas_call(functools.partial(backward_kernel, total_rows), out_shape=...]
    mul x0 -> x2, local copies, waits for them, and re-layouts: none -> 13.5 us  [norm_forward(): return ((values - col_mean[:, None, :]) * inv_std[:, None, :], inv_std)]
    sub x0 -> x2, local copies, waits for them, and re-layouts: none -> 13.5 us  [norm_forward(): return ((values - col_mean[:, None, :]) * inv_std[:, None, :], inv_std)]
    convert_element_type x0 -> x2, local copies, waits for them, and re-layouts: none -> 13 us  [the longest x1 6.53 us: local_step(): act_one = jax.nn.relu(pre_one).astype(BF16)]
    dot_general x0 -> x1, local copies, waits for them, and re-layouts: none -> 9.27 us  [local_step(): jnp.dot(feat_rows, w_one, preferred_element_type=F32)]
    unnamed x38 -> x27, local copies, waits for them, and re-layouts: 5.03 us -> 12.5 us
where the time goes in v2:
time: 502 us; the launch traced here: 494 us
  Pallas kernels  307 us (61%)
  matrix products  69.3 us (14%)
  local copies, waits for them, and re-layouts  68.2 us (14%)
  other arithmetic  47.9 us (10%)
    pallas_call x1, Pallas kernels, backward(): pl.pallas_call(functools.partial(backward_kernel, total_rows), out_shape=...  169 us
    pallas_call x1, Pallas kernels, corr_grad(): pl.pallas_call(functools.partial(corr_kernel, chunks, total_rows), out_sh...  97.6 us
    pallas_call x3, Pallas kernels, all_sums(): pl.pallas_call(sums_kernel, out_shape=jax.ShapeDtypeStruct(values.shape,...  39.8 us
    dot_general x1, matrix products, local_step(): hidden_two = jnp.dot(act_one, w_two, preferred_element_type=F32)  16.2 us
    dot_general x1, matrix products, local_step(): proj_out = jnp.dot(act_two, w_three, preferred_element_type=F32)  14.5 us
    mul x2, local copies, waits for them, and re-layouts, norm_forward(): return ((values - col_mean[:, None, :]) * inv_std[:, None, :], inv_std)  13.5 us
    sub x2, local copies, waits for them, and re-layouts, norm_forward(): return ((values - col_mean[:, None, :]) * inv_std[:, None, :], inv_std)  13.5 us
    dot_general x1, matrix products, local_step(): jnp.dot(feat_rows, w_one, preferred_element_type=F32)  13.4 us

profile of v2, /device:TPU:0, one launch (start us, length us, event | category | flops | bytes accessed | tf_op | source)
XLA Modules:
  0.0 493.8 jit_solution(6372913614018932819)
XLA Ops:
  1.3 2.9 copy.18
  4.2 3.9 copy.19
  8.1 4.3 fusion.18.feat_t
  12.5 0.0 copy-done.3
  12.5 13.4 %bitcast_reduce_fusion.1 = (f32[2,2048]{1,0:T(2,128)S(1)}, f32[2,2048]{1,0:T(2,128)S(1)}, f32[1024,2048]{1,0:T(8,128)}) fusion(bf16[2048,2048]{1,0:T(8,128)(2,1)} %param.12, bf16[512,2048]{0,1:T(8,128)(2,1)S(1)} %copy-done.3, bf16[512,2048]{0,1:T(8,128)(2,1)S(1)} %copy.18), kind=kOutput, calls=%fused_computation.10 | convolution fusion | flops 8604606464 | bytes 21004288 | tf_op jit(solution)/shard_map/dot_general | solution.py:628
  25.9 0.6 pad_maximum_fusion.4.in_ref
  26.5 15.1 %shard_map.161 = f32[4,2048]{1,0:T(4,128)} custom-call(f32[4,2048]{1,0:T(4,128)} %pad_maximum_fusion.4.in_ref), custom_call_target="tpu_custom_call" | custom-call | tf_op jit(solution)/shard_map/pallas_call | solution.py:81
  41.7 0.0 copy-done.6
  41.7 1.5 broadcast_multiply_fusion
  43.1 4.3 mul.92
  47.4 9.3 %copy.28 = f32[1024,2048]{0,1:T(8,128)} copy(f32[1024,2048]{1,0:T(8,128)} %bitcast.68) | data formatting | bytes 16777216 | tf_op jit(solution)/shard_map/mul | solution.py:618
  56.7 4.3 sub.39
  60.9 9.3 %copy.27 = f32[1024,2048]{0,1:T(8,128)} copy(f32[1024,2048]{1,0:T(8,128)} %bitcast.69) | data formatting | bytes 16777216 | tf_op jit(solution)/shard_map/sub | solution.py:618
  70.2 9.3 %copy.21 = f32[1024,2048]{0,1:T(8,128)} copy(f32[1024,2048]{1,0:T(8,128)} %get-tuple-element.48) | data formatting | bytes 16777216 | tf_op jit(solution)/shard_map/dot_general | solution.py:628
  79.5 0.0 copy-done.8
  79.5 12.6 %maximum_convert_fusion = (bf16[1024,2048]{0,1:T(8,128)(2,1)}, bf16[1024,2048]{0,1:T(8,128)(2,1)}) fusion(f32[2048]{0:T(1024)S(1)} %copy-done.8, f32[2048]{0:T(1024)S(1)} %copy-done.6, f32[1024,2048]{0,1:T(8,128)} %copy.28, f32[1024,2048]{0,1:T(8,128)} %copy.21, f32[1024,2048]{0,1:T(8,128)} %copy.27), kind=kLoop, calls=%fused_computation.17 | loop fusion | flops 14680064 | bytes 33570816 | tf_op jit(solution)/shard_map/convert_element_type | solution.py:631
  92.1 6.5 %copy.24.norm_one = bf16[1024,2048]{1,0:T(8,128)(2,1)} copy(bf16[1024,2048]{0,1:T(8,128)(2,1)} %get-tuple-element.37) | data formatting | bytes 8388608 | tf_op jit(solution)/shard_map/convert_element_type | solution.py:652
  98.5 16.2 %fusion.26 = (f32[2,2048]{1,0:T(2,128)S(1)}, f32[2,2048]{1,0:T(2,128)S(1)}, f32[2,512,2048]{2,1,0:T(8,128)}) fusion(bf16[2048,2048]{1,0:T(8,128)(2,1)} %w_two.1, f32[1024,2048]{1,0:T(8,128)} %get-tuple-element.48, f32[2048]{0:T(1024)S(1)} %copy-done.8, f32[2,2048]{1,0:T(2,128)S(1)} %get-tuple-element.33, f32[2,2048]{1,0:T(2,128)S(1)} %get-tuple-element.47, ...), kind=kOutput, calls=%fused_computation.59 | convolution fusion | flops 8608800768 | bytes 25247744 | tf_op jit(solution)/shard_map/dot_general | solution.py:632
  114.8 0.6 pad_maximum_fusion.5.in_ref
  115.4 12.8 %shard_map.162 = f32[4,2048]{1,0:T(4,128)} custom-call(f32[4,2048]{1,0:T(4,128)} %pad_maximum_fusion.5.in_ref), custom_call_target="tpu_custom_call" | custom-call | tf_op jit(solution)/shard_map/pallas_call | solution.py:81
  128.3 1.5 broadcast_multiply_fusion.1
  129.7 0.0 copy-done.7
  129.7 6.5 %fusion.11 = (bf16[2,512,2048]{2,1,0:T(8,128)(2,1)}, bf16[2,512,2048]{2,1,0:T(8,128)(2,1)}) fusion(f32[2,512,2048]{2,1,0:T(8,128)} %get-tuple-element.49, f32[2,2048]{1,0:T(2,128)S(1)} %get-tuple-element.35, f32[2,2048]{1,0:T(2,128)S(1)} %get-tuple-element.46, f32[2048]{0:T(1024)S(1)} %copy-done.7, f32[2048]{0:T(1024)S(1)} %copy-done.5), kind=kLoop, calls=%fused_computation.25 | loop fusion | flops 14680064 | bytes 16826368 | tf_op jit(solution)/shard_map/convert_element_type | solution.py:651
  136.2 6.4 %copy.29 = bf16[1024,2048]{0,1:T(8,128)(2,1)} copy(bf16[1024,2048]{1,0:T(8,128)(2,1)} %bitcast.63) | data formatting | bytes 8388608 | tf_op jit(solution)/shard_map/reshape | solution.py:648
  142.6 6.5 %copy.26.act_one = bf16[1024,2048]{1,0:T(8,128)(2,1)} copy(bf16[1024,2048]{0,1:T(8,128)(2,1)} %get-tuple-element.36) | data formatting | bytes 8388608 | tf_op jit(solution)/shard_map/convert_element_type | solution.py:631
  149.2 14.5 %fusion.25 = (f32[2,2048]{1,0:T(2,128)S(1)}, f32[2,2048]{1,0:T(2,128)S(1)}, f32[2,512,2048]{2,1,0:T(8,128)}) fusion(bf16[2,512,2048]{2,1,0:T(8,128)(2,1)} %get-tuple-element.39, bf16[2048,2048]{1,0:T(8,128)(2,1)} %w_three.1), kind=kOutput, calls=%fused_computation.58 | convolution fusion | flops 8596217856 | bytes 21004288 | tf_op jit(solution)/shard_map/dot_general | solution.py:636
  163.7 0.6 pad_maximum_fusion.6.in_ref
  164.3 11.9 %shard_map.163 = f32[4,2048]{1,0:T(4,128)} custom-call(f32[4,2048]{1,0:T(4,128)} %pad_maximum_fusion.6.in_ref), custom_call_target="tpu_custom_call" | custom-call | tf_op jit(solution)/shard_map/pallas_call | solution.py:81
  176.2 0.9 slice_multiply_fusion
  177.1 4.6 multiply_convert_fusion
  181.7 0.0 copy-start
  181.7 7.1 %convolution_convert_fusion = bf16[2048,2048]{1,0:T(8,128)(2,1)} fusion(bf16[2,512,2048]{2,1,0:T(8,128)(2,1)S(1)} %multiply_convert_fusion), kind=kOutput, calls=%fused_computation.24 | convolution fusion | flops 4299161600 | bytes 12582912 | tf_op jit(solution)/shard_map/dot_general | solution.py:639
  188.8 97.6 %shard_map.164 = (bf16[4,2,2,2,64,2048]{5,4,3,2,1,0:T(8,128)(2,1)}, f32[1,2048]{1,0:T(1,128)S(1)}) custom-call(bf16[4,2,2,2,64,2048]{5,4,3,2,1,0:T(8,128)(2,1)} %bitcast.73, f32[1]{0:T(128)} %bitcast.62.lam_ref), custom_call_target="tpu_custom_call" | custom-call | tf_op jit(solution)/shard_map/pallas_call | solution.py:234
  286.4 0.0 slice-start.1
  286.4 7.1 %fusion.21 = f32[512,2048]{1,0:T(8,128)S(1)} fusion(bf16[2048,2048]{1,0:T(8,128)(2,1)} %bitcast.78, bf16[2,512,2048]{2,1,0:T(8,128)(2,1)S(1)} %multiply_convert_fusion), kind=kOutput, calls=%fused_computation.37 | convolution fusion | flops 4294967296 | bytes 14680064 | tf_op jit(solution)/shard_map/dot_general | solution.py:643
  293.5 11.0 %fusion.20 = f32[512,2048]{1,0:T(8,128)} fusion(bf16[2048,2048]{1,0:T(8,128)(2,1)} %bitcast.79, bf16[2,512,2048]{2,1,0:T(8,128)(2,1)S(1)} %multiply_convert_fusion), kind=kOutput, calls=%fused_computation.36 | convolution fusion | flops 4294967296 | bytes 14680064 | tf_op jit(solution)/shard_map/dot_general | solution.py:641
  304.5 0.0 copy-done.1
  304.5 0.0 copy-start.2
  304.5 3.9 bitcast_reduce_fusion
  308.5 0.0 copy-done.2
  308.5 6.5 %pad_maximum_fusion.grad_embed = f32[1024,2048]{1,0:T(8,128)} fusion(f32[512,2048]{1,0:T(8,128)} %copy-done.1, f32[512,2048]{1,0:T(8,128)S(1)} %copy-done.2), kind=kLoop, calls=%fused_computation | loop fusion | flops 2097152 | bytes 16777216 | tf_op jit(solution)/shard_map/concatenate | solution.py:644
  315.0 0.7 pad_maximum_fusion.3.embed_sums
  315.6 169.1 %shard_map.165 = (f32[64,2048]{1,0:T(8,128)}, f32[64,2048]{1,0:T(8,128)}, f32[64,2048]{1,0:T(8,128)}, f32[5,2048]{1,0:T(8,128)}, f32[2,4,1024]{2,1,0:T(4,128)}, /*index=5*/f32[2,4,1024]{2,1,0:T(4,128)}) custom-call(f32[5,2048]{1,0:T(8,128)} %pad_maximum_fusion.3.embed_sums, f32[1024,2048]{1,0:T(8,128)} %pad_maximum_fusion.grad_embed, ...), custom_call_target="tpu_custom_call" | custom-call | tf_op jit(solution)/shard_map/pallas_call | solution.py:599
  484.7 1.5 slice_reduce_fusion
  486.2 1.6 slice_add_fusion
  487.8 1.9 copy.34
  489.6 1.9 copy.35
  491.5 1.9 copy.36
  (14 shorter events, 0.0 us)
Async XLA Ops:
  8.1 4.4 copy-start.3
  12.5 29.2 %copy-start.6 = (f32[2048]{0:T(1024)S(1)}, f32[2048]{0:T(1024)}, u32[]{:S(2)}) copy-start(f32[2048]{0:T(1024)} %param.15) | copy-start | bytes 24580
  70.2 9.3 %copy-start.8 = (f32[2048]{0:T(1024)S(1)}, f32[2048]{0:T(1024)}, u32[]{:S(2)}) copy-start(f32[2048]{0:T(1024)} %param.16) | copy-start | bytes 24580
  98.5 29.7 %copy-start.5 = (f32[2048]{0:T(1024)S(1)}, f32[2048]{0:T(1024)}, u32[]{:S(2)}) copy-start(f32[2048]{0:T(1024)} %param.17) | copy-start | bytes 24580
  98.5 31.2 %copy-start.7 = (f32[2048]{0:T(1024)S(1)}, f32[2048]{0:T(1024)}, u32[]{:S(2)}) copy-start(f32[2048]{0:T(1024)} %param.18) | copy-start | bytes 24580
  177.1 127.4 %copy-start.4 = (f32[2,2048]{1,0:T(2,128)}, f32[2,2048]{1,0:T(2,128)S(1)}, u32[]{:S(2)}) copy-start(f32[2,2048]{1,0:T(2,128)S(1)} %get-tuple-element.45.scale_three) | copy-start | bytes 49156
  181.7 111.8 %copy-start = (bf16[2,512,2048]{2,1,0:T(8,128)(2,1)}, bf16[2,512,2048]{2,1,0:T(8,128)(2,1)S(1)}, u32[]{:S(2)}) copy-start(bf16[2,512,2048]{2,1,0:T(8,128)(2,1)S(1)} %multiply_convert_fusion) | copy-start | bytes 12582916
  188.7 115.8 %slice-start = ((s8[8388608]{0:T(1024)(128)(4,1)}), s8[4194304]{0:T(1024)(128)(4,1)S(1)}, s32[]{:S(2)}) async-start(s8[8388608]{0:T(1024)(128)(4,1)} %bitcast.66), calls=%async_computation | async-start | bytes 8388608
  286.4 18.1 %slice-start.1 = ((s8[8388608]{0:T(1024)(128)(4,1)}), s8[4194304]{0:T(1024)(128)(4,1)S(1)}, s32[]{:S(2)}) async-start(s8[8388608]{0:T(1024)(128)(4,1)} %bitcast.66), calls=%async_computation.1 | async-start | bytes 8388608
  293.5 11.0 %copy-start.1 = (f32[512,2048]{1,0:T(8,128)}, f32[512,2048]{1,0:T(8,128)S(1)}, u32[]{:S(2)}) copy-start(f32[512,2048]{1,0:T(8,128)S(1)} %fusion.21) | copy-start | bytes 12582916
  304.5 4.0 copy-start.2

commit v3 on v2

--- a/solution.py
+++ b/solution.py
@@ -8,7 +8,6 @@
 from jax.sharding import PartitionSpec as P
 
 NORM_EPS = 1e-5
-FIRST_DIMS = (((0,), (0,)), ((), ()))
 MESH = pl.DeviceIdType.MESH
 F32 = jnp.float32
 BF16 = jnp.bfloat16
@@ -45,55 +44,6 @@
         device_id=(peer,), device_id_type=MESH)
 
 
-def sums_kernel(in_ref, out_ref, recv0, slots1, slots2, send_sem, recv_sem):
-    at = Place()
-    half = in_ref.shape[1] // 2
-    enter([at.partner] + at.plane_peers + at.z_peers)
-    mine = pl.ds(pl.multiple_of(at.core * half, 128), half)
-    theirs = pl.ds(pl.multiple_of((1 - at.core) * half, 128), half)
-    first = remote(in_ref.at[:, theirs], recv0, send_sem.at[0], recv_sem.at[0], at.partner)
-    first.start()
-    first.wait()
-    slots1[at.plane] = in_ref[:, mine] + recv0[...]
-    copies = []
-    for d in range(3):
-        copies.append(remote(slots1.at[at.plane], slots1.at[at.plane], send_sem.at[1 + d], recv_sem.at[1 + d],
-                             at.plane_peers[d]))
-        copies[-1].start()
-    for copy in copies:
-        copy.wait()
-    slots2[at.z] = (slots1[0] + slots1[1]) + (slots1[2] + slots1[3])
-    copies = []
-    for d in range(3):
-        copies.append(remote(slots2.at[at.z], slots2.at[at.z], send_sem.at[4 + d], recv_sem.at[4 + d],
-                             at.z_peers[d]))
-        copies[-1].start()
-    for copy in copies:
-        copy.wait()
-    out_ref[:, mine] = (slots2[0] + slots2[1]) + (slots2[2] + slots2[3])
-    last = remote(out_ref.at[:, mine], out_ref.at[:, mine], send_sem.at[7], recv_sem.at[7], at.partner)
-    last.start()
-    last.wait()
-
-
-def all_sums(values, collective_id):
-    rows, cols = values.shape
-    return pl.pallas_call(
-        sums_kernel,
-        out_shape=jax.ShapeDtypeStruct(values.shape, F32),
-        in_specs=[pl.BlockSpec(memory_space=pltpu.VMEM)],
-        out_specs=pl.BlockSpec(memory_space=pltpu.VMEM),
-        scratch_shapes=[
-            pltpu.VMEM((rows, cols // 2), F32),
-            pltpu.VMEM((4, rows, cols // 2), F32),
-            pltpu.VMEM((4, rows, cols // 2), F32),
-            pltpu.SemaphoreType.DMA((8,)),
-            pltpu.SemaphoreType.DMA((8,)),
-        ],
-        compiler_params=pltpu.CompilerParams(collective_id=collective_id, has_side_effects=True),
-    )(values)
-
-
 class Scatter:
     def __init__(self, at, part, bufs, send_sem, recv_sem, chunk):
         self.at, self.part, self.chunk = at, part, chunk
@@ -245,46 +195,57 @@
 
 class Sums:
     def __init__(self, at, local, total, recv0, slots1, slots2, send_sem, recv_sem):
-        self.at, self.local, self.total = at, local, total
+        self.at, self.refs = at, (local, total)
         self.recv0, self.slots1, self.slots2 = recv0, slots1, slots2
         self.send_sem, self.recv_sem = send_sem, recv_sem
-        half = local.shape[-1] // 2
-        self.mine = pl.ds(pl.multiple_of(at.core * half, 128), half)
-        self.theirs = pl.ds(pl.multiple_of((1 - at.core) * half, 128), half)
-        self.copies = []
-
-    def start(self, k, src, dst, peer):
-        copy = remote(src, dst, self.send_sem.at[k], self.recv_sem.at[k], peer)
-        copy.start()
-        self.copies.append(copy)
-
-    def arrive(self):
-        for copy in self.copies:
+        self.half = recv0.shape[-1]
+        self.mine = pl.multiple_of(at.core * self.half, 128)
+        self.theirs = pl.multiple_of((1 - at.core) * self.half, 128)
+
+    def pick(self, k, first):
+        ref, index = self.refs[k]
+        return ref.at[(*index, slice(None), pl.ds(first, self.half))]
+
+    def copies(self, stage):
+        at = self.at
+        if stage == 0:
+            pairs = [(0, self.pick(0, self.theirs), self.recv0, at.partner)]
+        elif stage == 1:
+            here = self.slots1.at[at.plane]
+            pairs = [(1 + d, here, here, at.plane_peers[d]) for d in range(3)]
+        elif stage == 2:
+            here = self.slots2.at[at.z]
+            pairs = [(4 + d, here, here, at.z_peers[d]) for d in range(3)]
+        else:
+            here = self.pick(1, self.mine)
+            pairs = [(7, here, here, at.partner)]
+        return [remote(src, dst, self.send_sem.at[k], self.recv_sem.at[k], peer) for k, src, dst, peer in pairs]
+
+    def send(self, stage):
+        for copy in self.copies(stage):
+            copy.start()
+
+    def arrive(self, stage=3):
+        for copy in self.copies(stage):
             copy.wait()
-        self.copies = []
 
     def begin(self):
-        self.start(0, self.local.at[:, self.theirs], self.recv0, self.at.partner)
+        self.send(0)
 
     def over_plane(self):
-        self.arrive()
-        here = self.slots1.at[self.at.plane]
-        here[...] = self.local[:, self.mine] + self.recv0[...]
-        for d in range(3):
-            self.start(1 + d, here, here, self.at.plane_peers[d])
+        self.arrive(0)
+        self.slots1[self.at.plane] = self.pick(0, self.mine)[...] + self.recv0[...]
+        self.send(1)
 
     def over_line(self):
-        self.arrive()
-        here = self.slots2.at[self.at.z]
-        here[...] = (self.slots1[0] + self.slots1[1]) + (self.slots1[2] + self.slots1[3])
-        for d in range(3):
-            self.start(4 + d, here, here, self.at.z_peers[d])
+        self.arrive(1)
+        self.slots2[self.at.z] = (self.slots1[0] + self.slots1[1]) + (self.slots1[2] + self.slots1[3])
+        self.send(2)
 
     def over_pair(self):
-        self.arrive()
-        here = self.total.at[:, self.mine]
-        here[...] = (self.slots2[0] + self.slots2[1]) + (self.slots2[2] + self.slots2[3])
-        self.start(7, here, here, self.at.partner)
+        self.arrive(2)
+        self.pick(1, self.mine)[...] = (self.slots2[0] + self.slots2[1]) + (self.slots2[2] + self.slots2[3])
+        self.send(3)
 
 
 def sums_scratch(rows, cols):
@@ -413,11 +374,11 @@
     outs = [grad_w_three, grad_w_two, grad_w_one]
     totals = [total_three, total_two, total_one]
     sums = {}
-    sums[0, 0] = Sums(at, embed_sums, total_three, *scratch[RING:RING + SUMS])
+    sums[0, 0] = Sums(at, (embed_sums, ()), (total_three, ()), *scratch[RING:RING + SUMS])
     for layer in (1, 2):
         for h in range(2):
             first = RING + SUMS * (2 * layer - 1 + h)
-            sums[layer, h] = Sums(at, local.at[layer - 1, h], totals[layer].at[h], *scratch[first:first + SUMS])
+            sums[layer, h] = Sums(at, (local, (layer - 1, h)), (totals[layer], (h,)), *scratch[first:first + SUMS])
 
     def load(src, dst, k):
         copy = pltpu.make_async_copy(src, dst, load_sem.at[k])
@@ -501,10 +462,10 @@
             ring.first(q)
         if 0 <= q - 2 <= last:
             ring.second(q - 2)
-        if 0 <= q - 3 <= last:
-            ring.third(q - 3)
-        if 0 <= q - 5 <= last:
-            done = q - 5
+        if 0 <= q - 4 <= last:
+            ring.third(q - 4)
+        if 0 <= q - 6 <= last:
+            done = q - 6
             outs[done // CHUNKS][:, pl.ds((done % CHUNKS) * width, width)] = ring.last(done)
 
     for layer in range(3):
@@ -573,7 +534,7 @@
         weight_grad(layer, 7)
         sums[layer + 1, 1].over_line()
         serve(q + 7)
-    for q in range(3 * CHUNKS, 3 * CHUNKS + 5):
+    for q in range(3 * CHUNKS, 3 * CHUNKS + 6):
         serve(q)
 
 
@@ -609,13 +570,178 @@
     )(*args)
 
 
-def norm_forward(values, total_rows, collective_id):
-    cols = values.shape[-1]
-    col_sums = jnp.concatenate([jnp.sum(values, axis=1), jnp.sum(values * values, axis=1)])
-    col_sums = all_sums(col_sums, collective_id).reshape(2, 2, cols)
-    col_mean = col_sums[0] / total_rows
-    inv_std = lax.rsqrt(col_sums[1] / total_rows - col_mean * col_mean + NORM_EPS)
-    return (values - col_mean[:, None, :]) * inv_std[:, None, :], inv_std
+def forward_kernel(
+        total_rows, feat_a, feat_b, w_one, w_two, w_three, gain_one, shift_one, gain_two, shift_two,
+        act_one, act_two, norm_one, norm_two, embed, feat_t, act_one_t, act_two_t, embed_t, scale_one, scale_two, scale_three,
+        acts, hidden, normed, turned, weight, local, total, w_sem, in_sem, out_sem, *scratch):
+    at = Place()
+    view_rows, dim = acts.shape[2:]
+    width = dim // CHUNKS
+    quarter = dim // 4
+    block_rows = min(64, view_rows)
+    weights = [w_one, w_two, w_three]
+    gains, shifts = [gain_one, gain_two], [shift_one, shift_two]
+    scales = [scale_one, scale_two, scale_three]
+    natural, normals, turns = [act_one, act_two, embed], [norm_one, norm_two], [feat_t, act_one_t, act_two_t, embed_t]
+    sums = {(layer, v): Sums(at, (local, (layer, v)), (total, (layer, v)), *scratch[SUMS * k:SUMS * k + SUMS])
+            for k, (layer, v) in enumerate((layer, v) for layer in range(3) for v in range(2))}
+
+    ins = [pltpu.make_async_copy((feat_a, feat_b)[v], acts.at[0, v], in_sem.at[v]) for v in range(2)]
+
+    def weight_copy(layer, k):
+        cols = pl.ds(k * quarter, quarter)
+        return pltpu.make_async_copy(weights[layer].at[:, cols], weight.at[layer % 2, :, cols], w_sem.at[layer % 2, k])
+
+    def load_weight(layer, k):
+        weight_copy(layer, k).start()
+
+    ins[0].start()
+    load_weight(0, 0)
+    ins[1].start()
+    for k in range(1, 4):
+        load_weight(0, k)
+    for k in range(4):
+        load_weight(1, k)
+    outs = {}
+
+    def put(name, v, src, dst, k):
+        copy = pltpu.make_async_copy(src, dst, out_sem.at[k, v])
+        copy.start()
+        outs[name, v] = copy
+
+    def drain(name, v):
+        outs.pop((name, v)).wait()
+
+    def matmul(layer, v, hooks=()):
+        hooks = list(hooks)
+        if v == 0:
+            hooks += [(2 * k, lambda k=k: weight_copy(layer, k).wait()) for k in range(4)]
+
+        @pl.loop(0, CHUNKS)
+        def _(n):
+            for k, step in hooks:
+                pl.when(n == k)(step)
+            cols = pl.ds(pl.multiple_of(n * width, width), width)
+            out = jnp.dot(acts[layer % 2, v], weight[layer % 2, :, cols], preferred_element_type=F32)
+            hidden[v, :, cols] = out
+            local[layer, v, 0:1, cols] = jnp.sum(out, axis=0, keepdims=True)
+            local[layer, v, 1:2, cols] = jnp.sum(out * out, axis=0, keepdims=True)
+
+    def normalise(layer, v):
+        mean = total[layer, v, 0:1, :] / total_rows
+        inv = lax.rsqrt(total[layer, v, 1:2, :] / total_rows - mean * mean + NORM_EPS)
+        if layer < 2:
+            scales[layer][v:v + 1, :] = gains[layer][...] * inv
+        else:
+            scales[layer][v:v + 1, :] = inv
+        local[layer, v, 0:1, :] = mean
+        local[layer, v, 1:2, :] = inv
+
+        @pl.loop(0, CHUNKS)
+        def _(n):
+            cols = pl.ds(pl.multiple_of(n * width, width), width)
+            mean, inv = local[layer, v, 0:1, cols], local[layer, v, 1:2, cols]
+            if layer < 2:
+                gain, shift = gains[layer][:, cols], shifts[layer][:, cols]
+
+            @pl.loop(0, view_rows // block_rows)
+            def _(r):
+                rows = pl.ds(pl.multiple_of(r * block_rows, block_rows), block_rows)
+                value = (hidden[v, rows, cols] - mean) * inv
+                if layer < 2:
+                    normed[v, rows, cols] = value.astype(BF16)
+                    value = jnp.maximum(gain * value + shift, 0.0)
+                acts[(layer + 1) % 2, v, rows, cols] = value.astype(BF16)
+
+        put(("act", layer), v, acts.at[(layer + 1) % 2, v], natural[layer].at[v], layer % 2)
+        if layer < 2:
+            put(("norm", layer), v, normed.at[v], normals[layer].at[v], 2)
+
+    def turn(k, v):
+        @pl.loop(0, CHUNKS)
+        def _(n):
+            cols = pl.ds(pl.multiple_of(n * width, width), width)
+            turned[cols, v * view_rows:(v + 1) * view_rows] = acts[k % 2, v, :, cols].T
+
+        span = pl.ds(v * view_rows, view_rows)
+        dst = turns[k].at[:, span] if k < 3 else turns[k]
+        put(("turn", k), v, turned.at[:, span], dst, 3)
+
+    enter([at.partner] + at.plane_peers + at.z_peers)
+    ins[0].wait()
+    matmul(0, 0)
+    sums[0, 0].begin()
+    ins[1].wait()
+    matmul(0, 1, [(2, sums[0, 0].over_plane), (7, sums[0, 0].over_line)])
+    sums[0, 1].begin()
+    turn(0, 0)
+    sums[0, 1].over_plane()
+    turn(0, 1)
+    for layer in range(3):
+        sums[layer, 0].over_pair()
+        if layer == 0:
+            for k in range(4):
+                load_weight(2, k)
+        sums[layer, 0].arrive()
+        for v in range(2):
+            if layer > 0:
+                if layer < 2:
+                    drain(("norm", layer - 1), v)
+                if layer == 2:
+                    drain(("act", 0), v)
+        normalise(layer, 0)
+        if layer < 2:
+            matmul(layer + 1, 0, [(0, sums[layer, 1].over_line), (7, sums[layer, 1].over_pair)])
+            sums[layer + 1, 0].begin()
+            sums[layer, 1].arrive()
+            normalise(layer, 1)
+            matmul(layer + 1, 1, [(0, sums[layer + 1, 0].over_plane), (6, sums[layer + 1, 0].over_line)])
+            sums[layer + 1, 1].begin()
+            drain(("turn", layer), 0)
+            turn(layer + 1, 0)
+            sums[layer + 1, 1].over_plane()
+            drain(("turn", layer), 1)
+            turn(layer + 1, 1)
+        else:
+            drain(("turn", 2), 0)
+            turn(3, 0)
+            sums[2, 1].over_line()
+            sums[2, 1].over_pair()
+            sums[2, 1].arrive()
+            normalise(2, 1)
+    for copy in outs.values():
+        copy.wait()
+
+
+def forward(total_rows, vmem, feat_a, feat_b, weights, vectors):
+    view_rows, dim = feat_a.shape
+    hbm = pl.BlockSpec(memory_space=pl.ANY)
+    vm = pl.BlockSpec(memory_space=pltpu.VMEM)
+    scratch = [
+        pltpu.VMEM((2, 2, view_rows, dim), BF16),
+        pltpu.VMEM((2, view_rows, dim), F32),
+        pltpu.VMEM((2, view_rows, dim), BF16),
+        pltpu.VMEM((dim, 2 * view_rows), BF16),
+        pltpu.VMEM((2, dim, dim), BF16),
+        pltpu.VMEM((3, 2, 2, dim), F32),
+        pltpu.VMEM((3, 2, 2, dim), F32),
+        pltpu.SemaphoreType.DMA((2, 4)),
+        pltpu.SemaphoreType.DMA((2,)),
+        pltpu.SemaphoreType.DMA((4, 2)),
+    ]
+    for _ in range(6):
+        scratch += sums_scratch(2, dim)
+    pair = jax.ShapeDtypeStruct((2, view_rows, dim), BF16)
+    turned = jax.ShapeDtypeStruct((dim, 2 * view_rows), BF16)
+    vector = jax.ShapeDtypeStruct((2, dim), F32)
+    return pl.pallas_call(
+        functools.partial(forward_kernel, total_rows),
+        out_shape=[pair] * 5 + [turned] * 3 + [jax.ShapeDtypeStruct((dim, view_rows), BF16)] + [vector] * 3,
+        in_specs=[hbm] * 5 + [vm] * 4,
+        out_specs=[hbm] * 9 + [vm] * 3,
+        scratch_shapes=scratch,
+        compiler_params=pltpu.CompilerParams(collective_id=0, has_side_effects=True, vmem_limit_bytes=vmem),
+    )(feat_a, feat_b, *weights, *[value.reshape(1, dim) for value in vectors])
 
 
 def solution(mesh):
@@ -624,19 +750,10 @@
     def local_step(h_a, h_b, w_one, w_two, w_three, gain_one, shift_one, gain_two, shift_two, lam_off):
         rows_dev = h_a.shape[0]
         total_rows = rows_dev * shards
-        feat_rows = jnp.concatenate([h_a, h_b], axis=0)
-        hidden_one = jnp.dot(feat_rows, w_one, preferred_element_type=F32).reshape(2, rows_dev, -1)
-        normed_one, inv_one = norm_forward(hidden_one, total_rows, 0)
-        pre_one = gain_one * normed_one + shift_one
-        act_one = jax.nn.relu(pre_one).astype(BF16)
-        hidden_two = jnp.dot(act_one, w_two, preferred_element_type=F32)
-        normed_two, inv_two = norm_forward(hidden_two, total_rows, 1)
-        pre_two = gain_two * normed_two + shift_two
-        act_two = jax.nn.relu(pre_two).astype(BF16)
-        proj_out = jnp.dot(act_two, w_three, preferred_element_type=F32)
-        normed_out, inv_out = norm_forward(proj_out, total_rows, 2)
-        embed_pair = normed_out.astype(BF16)
-        corr_part = lax.dot_general(embed_pair[0], embed_pair[1], FIRST_DIMS, preferred_element_type=F32)
+        (act_one, act_two, norm_one, norm_two, embed_pair, feat_t, act_one_t, act_two_t, embed_t,
+         scale_one, scale_two, scale_three) = forward(
+            total_rows, 56 * 2**20, h_a, h_b, (w_one, w_two, w_three), (gain_one, shift_one, gain_two, shift_two))
+        corr_part = jnp.dot(embed_t, embed_pair[1], preferred_element_type=F32)
         grad_scaled, loss_cols = corr_grad(corr_part.astype(BF16), lam_off, total_rows, 3)
         grad_embed_a = lax.dot_general(embed_pair[1], grad_scaled, (((1,), (1,)), ((), ())),
                                        preferred_element_type=F32)
@@ -646,11 +763,10 @@
         embed_sums = jnp.concatenate(
             [jnp.sum(products, axis=1), jnp.sum(products * embed_pair.astype(F32), axis=1), loss_cols])
         flat = lambda values: values.reshape(2 * rows_dev, -1)
-        act_one, act_two = flat(act_one), flat(act_two)
         grad_w_three, grad_w_two, grad_w_one, total_three, total_two, total_one = backward(
-            total_rows, 62 * 2**20, embed_sums, grad_embed, flat(embed_pair), flat(normed_two.astype(BF16)),
-            flat(normed_one.astype(BF16)), act_two, act_one, act_two.T, act_one.T, feat_rows.T, w_three, w_two,
-            inv_out, gain_two * inv_two, gain_one * inv_one)
+            total_rows, 62 * 2**20, embed_sums, grad_embed, flat(embed_pair), flat(norm_two), flat(norm_one),
+            flat(act_two), flat(act_one), act_two_t, act_one_t, feat_t, w_three, w_two,
+            scale_three, scale_two, scale_one)
         loss_total = jnp.sum(total_three[4])
         both = lambda total, row: (total[:, row] + total[:, row + 1]).reshape(-1)
         return (loss_total, grad_w_one, grad_w_two, grad_w_three,

time: 502 us -> 378 us (0.75)
  local copies, waits for them, and re-layouts: 68.2 us -> 5.62 us
  matrix products: 69.3 us -> 23.9 us
  other arithmetic: 47.9 us -> 9.19 us
  Pallas kernels: 307 us -> 334 us
    dot_general x4 -> x1, matrix products: 51.2 us -> 9.97 us  [local_step(): corr_part = jnp.dot(embed_t, embed_pair[1], preferred_element_type=F32)]
    pallas_call x3 -> x1, Pallas kernels: 39.8 us -> 72.1 us  [forward(): pl.pallas_call(functools.partial(forward_kernel, total_rows), out_shape=[...]
    convert_element_type x3 -> x0, other arithmetic: 23.7 us -> none  [the longest x1 12.6 us: local_step(): act_one = jax.nn.relu(pre_one).astype(BF16)]
    mul x2 -> x0, local copies, waits for them, and re-layouts: 13.5 us -> none  [norm_forward(): return ((values - col_mean[:, None, :]) * inv_std[:, None, :], inv_std)]
    sub x2 -> x0, local copies, waits for them, and re-layouts: 13.5 us -> none  [norm_forward(): return ((values - col_mean[:, None, :]) * inv_std[:, None, :], inv_std)]
    convert_element_type x2 -> x0, local copies, waits for them, and re-layouts: 13 us -> none  [the longest x1 6.53 us: local_step(): act_one = jax.nn.relu(pre_one).astype(BF16)]
    dot_general x1 -> x0, local copies, waits for them, and re-layouts: 9.27 us -> none  [local_step(): jnp.dot(feat_rows, w_one, preferred_element_type=F32)]
    unnamed x27 -> x5, local copies, waits for them, and re-layouts: 12.5 us -> 5.62 us
where the time goes in v3:
time: 378 us; the launch traced here: 375 us
  Pallas kernels  334 us (88%)
  matrix products  23.9 us (6%)
  other arithmetic  9.19 us (2%)
  local copies, waits for them, and re-layouts  5.62 us (1%)
    pallas_call x1, Pallas kernels, backward(): pl.pallas_call(functools.partial(backward_kernel, total_rows), out_shape=...  164 us
    pallas_call x1, Pallas kernels, corr_grad(): pl.pallas_call(functools.partial(corr_kernel, chunks, total_rows), out_sh...  97.8 us
    pallas_call x1, Pallas kernels, forward(): pl.pallas_call(functools.partial(forward_kernel, total_rows), out_shape=[...  72.1 us
    dot_general x1, matrix products, local_step(): corr_part = jnp.dot(embed_t, embed_pair[1], preferred_element_type=F32)  9.97 us

profile of v3, /device:TPU:0, one launch (start us, length us, event | category | flops | bytes accessed | tf_op | source)
XLA Modules:
  0.0 374.6 jit_solution(4895139236813944724)
XLA Ops:
  1.3 72.1 %shard_map.161 = (bf16[2,512,2048]{2,1,0:T(8,128)(2,1)}, bf16[2,512,2048]{2,1,0:T(8,128)(2,1)}, bf16[2,512,2048]{2,1,0:T(8,128)(2,1)}, bf16[2,512,2048]{2,1,0:T(...) custom-call(bf16[512,2048]{1,0:T(8,128)(2,1)} %feat_a.1, ...), custom_call_target="tpu_custom_call" | custom-call | tf_op jit(solution)/shard_map/pallas_call | solution.py:737
  73.4 10.0 %convolution_convert_fusion = bf16[2048,2048]{1,0:T(8,128)(2,1)} fusion(bf16[2048,512]{1,0:T(8,128)(2,1)} %get-tuple-element.29, bf16[2,512,2048]{2,1,0:T(8,128)(2,1)} %get-tuple-element.28), kind=kOutput, calls=%fused_computation.4 | convolution fusion | flops 4299161600 | bytes 12582912 | tf_op jit(solution)/shard_map/dot_general | solution.py:756
  83.3 0.0 copy-start
  83.3 97.8 %shard_map.162 = (bf16[4,2,2,2,64,2048]{5,4,3,2,1,0:T(8,128)(2,1)}, f32[1,2048]{1,0:T(1,128)S(1)}) custom-call(bf16[4,2,2,2,64,2048]{5,4,3,2,1,0:T(8,128)(2,1)} %bitcast.34, f32[1]{0:T(128)} %bitcast.32.lam_ref), custom_call_target="tpu_custom_call" | custom-call | tf_op jit(solution)/shard_map/pallas_call | solution.py:184
  181.1 0.0 copy-done
  181.1 6.9 %fusion.1 = f32[512,2048]{1,0:T(8,128)S(1)} fusion(bf16[2048,2048]{1,0:T(8,128)(2,1)} %bitcast.47, bf16[2,512,2048]{2,1,0:T(8,128)(2,1)S(1)} %copy-done), kind=kOutput, calls=%fused_computation.5 | convolution fusion | flops 4294967296 | bytes 14680064 | tf_op jit(solution)/shard_map/dot_general | solution.py:760
  188.1 7.0 %fusion.3 = f32[512,2048]{1,0:T(8,128)S(1)} fusion(bf16[2048,2048]{1,0:T(8,128)(2,1)} %bitcast.48, bf16[2,512,2048]{2,1,0:T(8,128)(2,1)S(1)} %copy-done), kind=kOutput, calls=%fused_computation.7 | convolution fusion | flops 4294967296 | bytes 14680064 | tf_op jit(solution)/shard_map/dot_general | solution.py:758
  195.0 1.7 bitcast_reduce_fusion
  196.7 3.8 %pad_maximum_fusion.grad_embed = f32[1024,2048]{1,0:T(8,128)} fusion(f32[512,2048]{1,0:T(8,128)S(1)} %fusion.1, f32[512,2048]{1,0:T(8,128)S(1)} %fusion.3), kind=kLoop, calls=%fused_computation | loop fusion | flops 2097152 | bytes 16777216 | tf_op jit(solution)/shard_map/concatenate | solution.py:761
  200.5 0.7 pad_maximum_fusion.1.embed_sums
  201.2 164.3 %shard_map.163 = (f32[64,2048]{1,0:T(8,128)}, f32[64,2048]{1,0:T(8,128)}, f32[64,2048]{1,0:T(8,128)}, f32[5,2048]{1,0:T(8,128)}, f32[2,4,1024]{2,1,0:T(4,128)}, /*index=5*/f32[2,4,1024]{2,1,0:T(4,128)}) custom-call(f32[5,2048]{1,0:T(8,128)} %pad_maximum_fusion.1.embed_sums, f32[1024,2048]{1,0:T(8,128)} %pad_maximum_fusion.grad_embed, ...), custom_call_target="tpu_custom_call" | custom-call | tf_op jit(solution)/shard_map/pallas_call | solution.py:560
  365.5 1.5 slice_reduce_fusion
  366.9 1.6 slice_add_fusion
  368.5 1.9 copy.22
  370.4 1.9 copy.23
  372.3 1.9 copy.24
Async XLA Ops:
  83.3 97.8 %copy-start = (bf16[2,512,2048]{2,1,0:T(8,128)(2,1)S(1)}, bf16[2,512,2048]{2,1,0:T(8,128)(2,1)}, u32[]{:S(2)}) copy-start(bf16[2,512,2048]{2,1,0:T(8,128)(2,1)} %get-tuple-element.28) | copy-start | bytes 12582916
